TPU v7x, 32 devices: a whole 2x2x4 slice. The times are simulated.
32 devices in a mesh: groups: 2 (over y), seq: 8 (over z, x), heads: 2 (over core).
Axes of the slice: x: 2, y: 2, z: 4, core: 2. Of those that a mesh axis runs over, the one named last changes fastest.
Arguments:
- queries: bfloat16 [2, 16, 16, 4096], P(None, ('groups', 'seq'), None, 'heads'), parts along dimension 1, may hold values from -8 to 8
- keys: bfloat16 [16, 4096, 512], P(('groups', 'seq'), None, 'heads'), parts along dimension 0, may hold values from -8 to 8
- values: bfloat16 [16, 4096, 512], P(('groups', 'seq'), None, 'heads'), parts along dimension 0, may hold values from -6 to 6
- tile_blocks: int32 [32, 4], P('groups'), parts along dimension 0, may hold values from 0 to 7, all different within a row; in each aligned block of 8 rows (0 to 7, 8 to 15, ...) at most 8 rows name the same one
- block_place: int32 [16], P('groups'), parts along dimension 0, may hold values from 0 to 7, each once
- tile_offset: int32 [32], P('groups'), parts along dimension 0, may hold values from 0 to 255
Outputs:
- attended: bfloat16 [2, 16, 16, 4096], P(None, ('groups', 'seq'), None, 'heads'), parts along dimension 1
There are 2 independent parts, one for each index of `groups`. A program takes and returns all parts, laid end to end along the dimension named above; each array names one. Nothing has to cross between parts.
Inputs may be any that keep to these rules, and one draw needn't show every extreme that they name: `tile_blocks`: each tile lists 4 different blocks; among the 8 tiles of one micro-batch no block is listed by more than 8 tiles, and in some micro-batch one block is listed by exactly 8. `block_place`: each index appears once.
All inputs are finite; a program needn't handle non-finite values.
Results may differ from a plain program's by a relative error of at most 0.0048.
Values may be sent and summed in bfloat16 or wider, within the bound.
No kernel may reach another device: no remote copies, remote signals or barrier semaphores. Data moves between devices by JAX's collectives and lax.ppermute only.
A program may use at most 128 MiB of HBM per device.

v0:
```python
import jax
import jax.numpy as jnp
from jax import lax
from jax.sharding import PartitionSpec as P

HEAD = 128
BLOCK = 4096
TOP = 4


def attend(tile_query, key_head, value_head, horizon):
    scores = jnp.einsum(
        "rgh,kh->grk", tile_query, key_head, preferred_element_type=jnp.float32
    ) * HEAD ** (-0.5)
    visible = jnp.arange(key_head.shape[0], dtype=jnp.int32)[None, :] <= horizon[:, None]
    scores = jnp.where(visible[None], scores, -1e30)
    highest = jnp.max(scores, axis=2, keepdims=True)
    weights = jnp.exp(scores - highest)
    summed = jnp.sum(weights, axis=2, keepdims=True)
    blended = (
        jnp.einsum(
            "grk,kh->grh",
            weights.astype(jnp.bfloat16),
            value_head,
            preferred_element_type=jnp.float32,
        )
        / summed
    )
    return (blended, (highest + jnp.log(summed))[..., 0])


def local(queries, keys, values, tile_blocks, block_place, tile_offset):
    seq_size = lax.axis_size("seq")
    my_index = lax.axis_index("seq")
    batch_total = queries.shape[0]
    tile_rows = queries.shape[2]
    features = queries.shape[3]
    shared_heads = keys.shape[2] // HEAD
    group_size = features // keys.shape[2]
    head_count = shared_heads * group_size
    block_count = block_place.shape[0]
    key_heads = keys[0].reshape(BLOCK, shared_heads, HEAD).transpose(1, 0, 2)
    value_heads = values[0].reshape(BLOCK, shared_heads, HEAD).transpose(1, 0, 2)
    block_ids = jnp.arange(block_count, dtype=jnp.int32)
    my_block = jnp.sum(jnp.where(block_place == my_index, block_ids, 0))
    device_ids = jnp.arange(seq_size, dtype=jnp.int32)
    all_owners = jnp.sum(
        jnp.where(
            tile_blocks[:, :, None] == block_ids[None, None, :], block_place[None, None, :], 0
        ),
        axis=2,
    )
    halves = []
    for batch_id in range(batch_total):
        first_row = batch_id * seq_size
        local_query = queries[batch_id : batch_id + 1]
        block_lists = tile_blocks[first_row : first_row + seq_size]
        owners = all_owners[first_row : first_row + seq_size]
        batch_here = local_query.shape[0]
        tile_count = block_lists.shape[0]
        capacity = batch_here * min(seq_size, 3 * TOP)
        is_mine = jnp.any(owners == my_index, axis=1)
        listed = is_mine.astype(jnp.int32)
        ordinal = jnp.cumsum(listed) - listed
        chosen = is_mine[:, None] & (
            ordinal[:, None] == jnp.arange(capacity, dtype=jnp.int32)[None, :]
        )
        tile_ids = jnp.arange(tile_count, dtype=jnp.int32)
        slot_tile = jnp.sum(jnp.where(chosen, tile_ids[:, None], 0), axis=0)
        slot_live = jnp.any(chosen, axis=0)
        tile_owners = owners.reshape(batch_here, seq_size, TOP)
        my_owners = lax.dynamic_index_in_dim(tile_owners, my_index, axis=1, keepdims=False)
        send_to = jnp.any(my_owners[:, :, None] == device_ids[None, None, :], axis=1)
        outgoing = jnp.where(send_to[:, :, None, None], local_query, jnp.zeros((), jnp.bfloat16))
        gathered = lax.all_to_all(outgoing, "seq", split_axis=1, concat_axis=1, tiled=True)
        flat_tiles = gathered.reshape(tile_count, tile_rows, features)
        arrived = jnp.einsum(
            "hm,hnq->mnq",
            chosen.astype(jnp.bfloat16),
            flat_tiles,
            preferred_element_type=jnp.float32,
        ).astype(jnp.bfloat16)
        own_slot = jnp.max(block_lists[slot_tile], axis=1) == my_block
        row_ids = jnp.arange(tile_rows, dtype=jnp.int32)
        horizons = jnp.where(
            own_slot[:, None],
            tile_offset[first_row : first_row + seq_size][slot_tile][:, None] * tile_rows
            + row_ids[None, :],
            BLOCK,
        )

        def one_slot(bundle):
            tile_query, horizon, live = bundle
            split_query = tile_query.reshape(tile_rows, shared_heads, group_size, HEAD).transpose(
                1, 0, 2, 3
            )

            def compute(unused):
                blended, mass = lax.map(
                    lambda heads_bundle: attend(
                        heads_bundle[0], heads_bundle[1], heads_bundle[2], horizon
                    ),
                    (split_query, key_heads, value_heads),
                )
                return (
                    blended.transpose(2, 0, 1, 3).reshape(tile_rows, features),
                    mass.transpose(2, 0, 1).reshape(tile_rows, head_count),
                )

            def nothing(unused):
                return (
                    jnp.zeros((tile_rows, features), jnp.float32),
                    jnp.zeros((tile_rows, head_count), jnp.float32),
                )

            return lax.cond(live, compute, nothing, 0)

        partial_out, partial_mass = lax.map(one_slot, (arrived, horizons, slot_live))
        target = jnp.where(slot_live, slot_tile, tile_count)
        out_rows = (
            jnp.zeros((tile_count, tile_rows, features), jnp.float32)
            .at[target]
            .set(partial_out, mode="drop")
        )
        out_mass = (
            jnp.zeros((tile_count, tile_rows, head_count), jnp.float32)
            .at[target]
            .set(partial_mass, mode="drop")
        )
        returned = lax.all_to_all(
            out_rows.reshape(batch_here, seq_size, tile_rows, features),
            "seq",
            split_axis=1,
            concat_axis=1,
            tiled=True,
        )
        returned_mass = lax.all_to_all(
            out_mass.reshape(batch_here, seq_size, tile_rows, head_count),
            "seq",
            split_axis=1,
            concat_axis=1,
            tiled=True,
        )
        batch_ids = jnp.arange(batch_here, dtype=jnp.int32)[:, None]
        pieces = returned[batch_ids, my_owners]
        masses = returned_mass[batch_ids, my_owners]
        highest = jnp.max(masses, axis=1, keepdims=True)
        weight_share = jnp.exp(masses - highest)
        weight_share = weight_share / jnp.sum(weight_share, axis=1, keepdims=True)
        blended = jnp.sum(jnp.repeat(weight_share, HEAD, axis=3) * pieces, axis=1)
        halves.append(blended[:, None].astype(jnp.bfloat16))
    return jnp.concatenate(halves, axis=0)


def solution(mesh):
    placed = (
        P(None, ("groups", "seq"), None, "heads"),
        P(("groups", "seq"), None, "heads"),
        P(("groups", "seq"), None, "heads"),
        P("groups", None),
        P("groups"),
        P("groups"),
    )
    return jax.shard_map(
        local,
        mesh=mesh,
        in_specs=placed,
        out_specs=P(None, ("groups", "seq"), None, "heads"),
        check_vma=False,
    )
```

profile of v0, /device:TPU:0, one launch (start us, length us, event | category | flops | bytes accessed | tf_op | source)
XLA Modules:
  0.0 307.6 jit_solution(1879499270316512934)
XLA Ops:
  3.5 7.3 %all-to-all-start = ((bf16[1,8,16,2048]{3,2,0,1:T(8,128)(2,1)}), bf16[1,8,16,2048]{3,2,0,1:T(8,128)(2,1)S(1)}, u32[]{:S(2)}, u32[]{:S(2)}) async-start(bf16[1,8,16,2048]{3,2,0,1:T(8,128)(2,1)} %broadcast_select_fusion.1), calls=%async_computation | async-start | bytes 1048576 | tf_op jit(solution)/shard_map/all_to_all | solution.py:75
  11.7 1.3 fusion.58
  15.0 1.2 fusion.59
  19.1 1.2 fusion.60
  20.3 2.9 copy.87
  23.3 2.5 copy.92
  25.7 4.1 %copy.88 = bf16[1,4096,256]{1,2,0:T(8,128)(2,1)} copy(bf16[1,4096,256]{2,1,0:T(8,128)(2,1)} %param.20) | data formatting | bytes 4194304 | tf_op args[2]
  29.8 3.1 %copy.93 = bf16[2,4096,128]{2,1,0:T(8,128)(2,1)S(1)} copy(bf16[2,4096,128]{1,2,0:T(8,128)(2,1)} %bitcast.241) | data formatting | bytes 4194304
  36.6 6.0 %all-to-all-start.3 = ((bf16[1,8,16,2048]{3,2,0,1:T(8,128)(2,1)}), bf16[1,8,16,2048]{3,2,0,1:T(8,128)(2,1)}, u32[]{:S(2)}, u32[]{:S(2)}) async-start(bf16[1,8,16,2048]{3,2,0,1:T(8,128)(2,1)} %broadcast_select_fusion), calls=%async_computation.3 | async-start | bytes 1048576 | tf_op jit(solution)/shard_map/all_to_all | solution.py:75
  43.0 1.1 copy.91
  44.2 46.7 %while.60 = (s32[]{:T(128)}, f32[8,16,2048]{2,1,0:T(8,128)S(1)}, f32[8,16,16]{2,1,0:T(8,128)S(1)}, pred[8]{0:T(512)(128)(4,1)}, bf16[8,16,2048]{2,1,0:T(8,128)(2...) while((s32[]{:T(128)}, f32[8,16,2048]{2,1,0:T(8,128)S(1)}, ...), condition=%wide.region_15.16_spmd.clone, body=%wide.region_8.15_spmd.clone.sunk | while | flops 272187520 | bytes 9769553 | solution.py:118
  45.1 1.3 dynamic_slice.93
  47.0 7.2 %conditional.6 = (f32[1,16,2048]{2,1,0:T(8,128)S(1)}, f32[1,16,16]{1,2,0:T(8,128)}) conditional(s32[]{:T(128)} %bitcast.223, () %tuple.136, (pred[8]{0:T(512)(128)(4,1)S(1)}, s32[]{:T(128)}, bf16[2,4096,128]{2,1,0:T(8,128)(2,1)}, bf16[2,16,8,128]{3,2,0,1:T(8,128)(2,1)S(1)}, bf16[2,4096,128]{2,1,0:T(8,128)(2,1)S(1)}, ...), branch_computations={%region_9.9_spmd, %region_10.14_spmd.clone} | conditional | flops 272187520 | bytes 9226141 | solution.py:116
  47.1 6.9 %while.58 = (s32[]{:T(128)}, f32[2,8,16,128]{3,2,1,0:T(8,128)S(1)}, f32[2,8,16]{2,1,0:T(8,128)}, s32[16]{0:T(128)S(1)}, bf16[2,4096,128]{2,1,0:T(8,128)(2,1)}, /...) while((s32[]{:T(128)}, f32[2,8,16,128]{3,2,1,0:T(8,128)S(1)}, ...), condition=%wide.region_14.13_spmd, body=%wide.region_11.12_spmd.sunk | while | flops 272187264 | bytes 8700569 | solution.py:99
  47.2 1.7 fusion.85
  50.7 1.7 fusion.85
  55.8 1.3 dynamic_slice.93
  57.7 7.2 %conditional.6 = (f32[1,16,2048]{2,1,0:T(8,128)S(1)}, f32[1,16,16]{1,2,0:T(8,128)}) conditional(s32[]{:T(128)} %bitcast.223, () %tuple.136, (pred[8]{0:T(512)(128)(4,1)S(1)}, s32[]{:T(128)}, bf16[2,4096,128]{2,1,0:T(8,128)(2,1)}, bf16[2,16,8,128]{3,2,0,1:T(8,128)(2,1)S(1)}, bf16[2,4096,128]{2,1,0:T(8,128)(2,1)S(1)}, ...), branch_computations={%region_9.9_spmd, %region_10.14_spmd.clone} | conditional | flops 272187520 | bytes 9226141 | solution.py:116
  57.9 6.9 %while.58 = (s32[]{:T(128)}, f32[2,8,16,128]{3,2,1,0:T(8,128)S(1)}, f32[2,8,16]{2,1,0:T(8,128)}, s32[16]{0:T(128)S(1)}, bf16[2,4096,128]{2,1,0:T(8,128)(2,1)}, /...) while((s32[]{:T(128)}, f32[2,8,16,128]{3,2,1,0:T(8,128)S(1)}, ...), condition=%wide.region_14.13_spmd, body=%wide.region_11.12_spmd.sunk | while | flops 272187264 | bytes 8700569 | solution.py:99
  58.0 1.7 fusion.85
  61.5 1.8 fusion.85
  66.6 1.3 dynamic_slice.93
  70.8 1.3 dynamic_slice.93
  75.0 1.3 dynamic_slice.93
  79.2 1.3 dynamic_slice.93
  83.4 1.3 dynamic_slice.93
  87.6 1.3 dynamic_slice.93
  92.5 44.3 %all-to-all-start.1 = ((f32[8,1,256]{2,1,0:T(1,128)}), f32[8,1,256]{2,1,0:T(1,128)S(1)}, u32[]{:S(2)}, u32[]{:S(2)}) async-start(f32[8,1,256]{2,1,0:T(1,128)} %reshape.624), calls=%async_computation.1 | async-start | bytes 16384 | tf_op jit(solution)/shard_map/all_to_all | solution.py:137
  136.8 1.5 convolution_convert_fusion
  139.4 1.1 broadcast.326.clone
  140.5 60.3 %while.61 = (s32[]{:T(128)}, f32[8,16,2048]{2,1,0:T(8,128)}, f32[8,16,16]{2,1,0:T(8,128)S(1)}, pred[8]{0:T(512)(128)(4,1)}, bf16[8,16,2048]{2,1,0:T(8,128)(2,1)}...) while((s32[]{:T(128)}, f32[8,16,2048]{2,1,0:T(8,128)}, ...), condition=%wide.region_34.35_spmd.clone, body=%wide.region_27.34_spmd.clone.sunk | while | flops 272187520 | bytes 9770061 | solution.py:118
  141.3 1.2 dynamic_slice.95
  143.2 7.8 %conditional.7 = (f32[1,16,2048]{2,1,0:T(8,128)S(1)}, f32[1,16,16]{1,2,0:T(8,128)}) conditional(s32[]{:T(128)} %bitcast.226, () %tuple.139, (pred[8]{0:T(512)(128)(4,1)S(1)}, s32[]{:T(128)}, bf16[2,4096,128]{2,1,0:T(8,128)(2,1)}, bf16[2,16,8,128]{3,2,0,1:T(8,128)(2,1)S(1)}, bf16[2,4096,128]{2,1,0:T(8,128)(2,1)S(1)}, /*index=5*/s32[8]{0:T(128)}, ...), branch_computations={%region_28.28_spmd, %region_29.33_spmd.clone} | conditional | flops 272187520 | bytes 9226141 | solution.py:116
  144.0 6.9 %while.59 = (s32[]{:T(128)}, f32[2,8,16,128]{3,2,1,0:T(8,128)S(1)}, f32[2,8,16]{2,1,0:T(8,128)}, s32[16]{0:T(128)S(1)}, bf16[2,4096,128]{2,1,0:T(8,128)(2,1)}, /...) while((s32[]{:T(128)}, f32[2,8,16,128]{3,2,1,0:T(8,128)S(1)}, ...), condition=%wide.region_33.32_spmd, body=%wide.region_30.31_spmd.sunk | while | flops 272187264 | bytes 8700569 | solution.py:99
  144.2 1.7 fusion.80
  147.7 1.7 fusion.80
  153.4 1.2 dynamic_slice.95
  155.3 7.8 %conditional.7 = (f32[1,16,2048]{2,1,0:T(8,128)S(1)}, f32[1,16,16]{1,2,0:T(8,128)}) conditional(s32[]{:T(128)} %bitcast.226, () %tuple.139, (pred[8]{0:T(512)(128)(4,1)S(1)}, s32[]{:T(128)}, bf16[2,4096,128]{2,1,0:T(8,128)(2,1)}, bf16[2,16,8,128]{3,2,0,1:T(8,128)(2,1)S(1)}, bf16[2,4096,128]{2,1,0:T(8,128)(2,1)S(1)}, /*index=5*/s32[8]{0:T(128)}, ...), branch_computations={%region_28.28_spmd, %region_29.33_spmd.clone} | conditional | flops 272187520 | bytes 9226141 | solution.py:116
  156.1 6.9 %while.59 = (s32[]{:T(128)}, f32[2,8,16,128]{3,2,1,0:T(8,128)S(1)}, f32[2,8,16]{2,1,0:T(8,128)}, s32[16]{0:T(128)S(1)}, bf16[2,4096,128]{2,1,0:T(8,128)(2,1)}, /...) while((s32[]{:T(128)}, f32[2,8,16,128]{3,2,1,0:T(8,128)S(1)}, ...), condition=%wide.region_33.32_spmd, body=%wide.region_30.31_spmd.sunk | while | flops 272187264 | bytes 8700569 | solution.py:99
  156.2 1.7 fusion.80
  159.7 1.7 fusion.80
  165.4 1.2 dynamic_slice.95
  167.3 7.8 %conditional.7 = (f32[1,16,2048]{2,1,0:T(8,128)S(1)}, f32[1,16,16]{1,2,0:T(8,128)}) conditional(s32[]{:T(128)} %bitcast.226, () %tuple.139, (pred[8]{0:T(512)(128)(4,1)S(1)}, s32[]{:T(128)}, bf16[2,4096,128]{2,1,0:T(8,128)(2,1)}, bf16[2,16,8,128]{3,2,0,1:T(8,128)(2,1)S(1)}, bf16[2,4096,128]{2,1,0:T(8,128)(2,1)S(1)}, /*index=5*/s32[8]{0:T(128)}, ...), branch_computations={%region_28.28_spmd, %region_29.33_spmd.clone} | conditional | flops 272187520 | bytes 9226141 | solution.py:116
  168.1 7.0 %while.59 = (s32[]{:T(128)}, f32[2,8,16,128]{3,2,1,0:T(8,128)S(1)}, f32[2,8,16]{2,1,0:T(8,128)}, s32[16]{0:T(128)S(1)}, bf16[2,4096,128]{2,1,0:T(8,128)(2,1)}, /...) while((s32[]{:T(128)}, f32[2,8,16,128]{3,2,1,0:T(8,128)S(1)}, ...), condition=%wide.region_33.32_spmd, body=%wide.region_30.31_spmd.sunk | while | flops 272187264 | bytes 8700569 | solution.py:99
  168.3 1.7 fusion.80
  171.8 1.7 fusion.80
  177.5 1.2 dynamic_slice.95
  182.3 1.2 dynamic_slice.95
  187.1 1.2 dynamic_slice.95
  192.0 1.2 dynamic_slice.95
  196.8 1.2 dynamic_slice.95
  202.4 41.2 %all-to-all-start.4 = ((f32[8,1,256]{2,1,0:T(1,128)}), f32[8,1,256]{2,1,0:T(1,128)S(1)}, u32[]{:S(2)}, u32[]{:S(2)}) async-start(f32[8,1,256]{2,1,0:T(1,128)} %reshape.622), calls=%async_computation.4 | async-start | bytes 16384 | tf_op jit(solution)/shard_map/all_to_all | solution.py:137
  243.5 1.1 broadcast.326.clone.3
  244.7 2.8 scatter_fusion.1
  247.5 2.6 all-to-all-done.4
  250.1 3.6 %all-to-all-start.2 = ((f32[1,8,16,2048]{3,2,0,1:T(8,128)}), f32[1,8,16,2048]{3,2,0,1:T(8,128)S(1)}, u32[]{:S(2)}, u32[]{:S(2)}) async-start(f32[1,8,16,2048]{3,2,0,1:T(8,128)} %bitcast.42), calls=%async_computation.2 | async-start | bytes 2097152 | tf_op jit(solution)/shard_map/all_to_all | solution.py:130
  253.7 1.1 broadcast.326.clone.1
  254.8 2.6 scatter_fusion.3
  257.4 20.0 %all-to-all-done.2 = f32[1,8,16,2048]{3,2,0,1:T(8,128)S(1)} async-done(((f32[1,8,16,2048]{3,2,0,1:T(8,128)}), f32[1,8,16,2048]{3,2,0,1:T(8,128)S(1)}, u32[]{:S(2)}, u32[]{:S(2)}) %all-to-all-start.2) | async-done | bytes 1048608 | tf_op jit(solution)/shard_map/all_to_all | solution.py:130
  277.4 3.6 %all-to-all-start.5 = ((f32[1,8,16,2048]{3,2,0,1:T(8,128)}), f32[1,8,16,2048]{3,2,0,1:T(8,128)S(1)}, u32[]{:S(2)}, u32[]{:S(2)}) async-start(f32[1,8,16,2048]{3,2,0,1:T(8,128)} %bitcast.62), calls=%async_computation.5 | async-start | bytes 2097152 | tf_op jit(solution)/shard_map/all_to_all | solution.py:130
  285.6 1.1 broadcast_in_dim.239
  286.8 1.4 gather_fusion.3
  288.2 1.1 fusion.34
  289.3 17.0 %all-to-all-done.5 = f32[1,8,16,2048]{3,2,0,1:T(8,128)S(1)} async-done(((f32[1,8,16,2048]{3,2,0,1:T(8,128)}), f32[1,8,16,2048]{3,2,0,1:T(8,128)S(1)}, u32[]{:S(2)}, u32[]{:S(2)}) %all-to-all-start.5) | async-done | bytes 1048608 | tf_op jit(solution)/shard_map/all_to_all | solution.py:130
  (294 shorter events, 88.5 us)
Async XLA Ops:
  3.5 33.0 %all-to-all-start = ((bf16[1,8,16,2048]{3,2,0,1:T(8,128)(2,1)}), bf16[1,8,16,2048]{3,2,0,1:T(8,128)(2,1)S(1)}, u32[]{:S(2)}, u32[]{:S(2)}) async-start(bf16[1,8,16,2048]{3,2,0,1:T(8,128)(2,1)} %broadcast_select_fusion.1), calls=%async_computation | async-start | bytes 1048576 | tf_op jit(solution)/shard_map/all_to_all | solution.py:75
  10.9 5.3 %copy-start.1 = (pred[8]{0:T(512)(128)(4,1)}, pred[8]{0:T(512)(128)(4,1)S(1)}, u32[]{:S(2)}) copy-start(pred[8]{0:T(512)(128)(4,1)S(1)} %get-tuple-element.464) | copy-start | bytes 28
  13.2 2.9 copy-start.3
  36.6 55.9 %all-to-all-start.3 = ((bf16[1,8,16,2048]{3,2,0,1:T(8,128)(2,1)}), bf16[1,8,16,2048]{3,2,0,1:T(8,128)(2,1)}, u32[]{:S(2)}, u32[]{:S(2)}) async-start(bf16[1,8,16,2048]{3,2,0,1:T(8,128)(2,1)} %broadcast_select_fusion), calls=%async_computation.3 | async-start | bytes 1048576 | tf_op jit(solution)/shard_map/all_to_all | solution.py:75
  92.5 109.9 %all-to-all-start.1 = ((f32[8,1,256]{2,1,0:T(1,128)}), f32[8,1,256]{2,1,0:T(1,128)S(1)}, u32[]{:S(2)}, u32[]{:S(2)}) async-start(f32[8,1,256]{2,1,0:T(1,128)} %reshape.624), calls=%async_computation.1 | async-start | bytes 16384 | tf_op jit(solution)/shard_map/all_to_all | solution.py:137
  202.4 47.7 %all-to-all-start.4 = ((f32[8,1,256]{2,1,0:T(1,128)}), f32[8,1,256]{2,1,0:T(1,128)S(1)}, u32[]{:S(2)}, u32[]{:S(2)}) async-start(f32[8,1,256]{2,1,0:T(1,128)} %reshape.622), calls=%async_computation.4 | async-start | bytes 16384 | tf_op jit(solution)/shard_map/all_to_all | solution.py:137
  247.5 7.3 %copy-start = (f32[8,16,2048]{2,1,0:T(8,128)S(1)}, f32[8,16,2048]{2,1,0:T(8,128)}, u32[]{:S(2)}) copy-start(f32[8,16,2048]{2,1,0:T(8,128)} %get-tuple-element.234) | copy-start | bytes 3145732
  247.5 7.3 %copy-start.2 = (s32[8]{0:T(128)S(1)}, s32[8]{0:T(128)}, u32[]{:S(2)}) copy-start(s32[8]{0:T(128)} %get-tuple-element.546) | copy-start | bytes 100
  250.1 27.3 %all-to-all-start.2 = ((f32[1,8,16,2048]{3,2,0,1:T(8,128)}), f32[1,8,16,2048]{3,2,0,1:T(8,128)S(1)}, u32[]{:S(2)}, u32[]{:S(2)}) async-start(f32[1,8,16,2048]{3,2,0,1:T(8,128)} %bitcast.42), calls=%async_computation.2 | async-start | bytes 2097152 | tf_op jit(solution)/shard_map/all_to_all | solution.py:130
  254.8 26.2 %copy-start.5 = (s32[4]{0:T(128)S(1)}, s32[4]{0:T(128)}, u32[]{:S(2)}) copy-start(s32[4]{0:T(128)} %get-tuple-element.461) | copy-start | bytes 52
  254.8 26.2 %copy-start.4 = (s32[4]{0:T(128)S(1)}, s32[4]{0:T(128)}, u32[]{:S(2)}) copy-start(s32[4]{0:T(128)} %get-tuple-element.550) | copy-start | bytes 52
  277.4 28.9 %all-to-all-start.5 = ((f32[1,8,16,2048]{3,2,0,1:T(8,128)}), f32[1,8,16,2048]{3,2,0,1:T(8,128)S(1)}, u32[]{:S(2)}, u32[]{:S(2)}) async-start(f32[1,8,16,2048]{3,2,0,1:T(8,128)} %bitcast.62), calls=%async_computation.5 | async-start | bytes 2097152 | tf_op jit(solution)/shard_map/all_to_all | solution.py:130
where the time goes:
time: 311 us; the launch traced here: 308 us
  starting transfers between devices  106 us (34%)
  local copies, waits for them, and re-layouts  96.9 us (31%)
  waiting for transfers between devices  39.6 us (13%)
  other arithmetic  28.6 us (9%)
  matrix products  24.8 us (8%)
  loops' own time  11.5 us (4%)
    all_to_all x2, starting transfers between devices, local(): lax.all_to_all(out_mass.reshape(batch_here, seq_size, tile_rows, head_cou...  85.5 us
    all_to_all x2, waiting for transfers between devices, local(): lax.all_to_all(out_rows.reshape(batch_here, seq_size, tile_rows, features...  37 us
    dynamic_slice x16, local copies, waits for them, and re-layouts, local(): lax.map(one_slot, (arrived, horizons, slot_live))  20 us
    dynamic_update_slice x48, local copies, waits for them, and re-layouts, local(): lax.map(one_slot, (arrived, horizons, slot_live))  17.7 us
    dot_general x10, matrix products, attend(): jnp.einsum('rgh,kh->grk', tile_query, key_head, preferred_element_type=jn...  17.5 us
    unnamed x26, local copies, waits for them, and re-layouts  16.5 us
    while x32, local copies, waits for them, and re-layouts  13.7 us
    all_to_all x2, starting transfers between devices, local(): lax.all_to_all(outgoing, 'seq', split_axis=1, concat_axis=1, tiled=True)  13.3 us
  transfers between devices with their start and end apart: 6, of which 3 were waited for; matrix products, arithmetic and copies ran while one was open for 47% of the time, Pallas kernels for 0%

commit v1 on v0

v1 whole, which is shorter than its diff:
```python
import functools

import jax
import jax.numpy as jnp
from jax import lax
from jax.experimental import pallas as pl
from jax.experimental.pallas import tpu as pltpu
from jax.sharding import PartitionSpec as P

HEAD = 128
SCALE = HEAD ** (-0.5) * 1.4426950408889634
KEYS = 256
STEP = 512
SMALL = 2.0**-60
LARGE = 2.0**100
PAD = 16


def prepare(me, tile_blocks, block_place, tile_offset, values, turned, slots, *, tile_rows):
    keys, features = values.shape
    for head in range(features // HEAD):
        for start in range(0, keys, 512):
            turned[head, :HEAD, start : start + 512] = values[
                start : start + 512, head * HEAD : (head + 1) * HEAD
            ].T
        turned[head, HEAD:, :] = jnp.where(
            lax.broadcasted_iota(jnp.int32, (PAD, keys), 0) == 0, 1.0, 0.0
        ).astype(turned.dtype)
    block_count = block_place.shape[0]
    tiles, top = tile_blocks.shape

    def find(block, mine):
        return jnp.where(block_place[block] == me[0], block, mine)

    mine = lax.fori_loop(0, block_count, find, 0)

    def visit(tile, count):
        entries = [tile_blocks[tile, entry] for entry in range(top)]
        own = functools.reduce(jnp.maximum, entries)
        named = functools.reduce(jnp.logical_or, [entry == mine for entry in entries])

        @pl.when(named)
        def _():
            slots[1 + count] = tile
            slots[1 + tiles + 1 + count] = jnp.where(
                own == mine, tile_offset[tile] * tile_rows, keys
            )

        return count + named.astype(jnp.int32)

    count = lax.fori_loop(0, tiles, visit, 0)
    slots[0] = count

    @pl.when(count % 2 == 1)
    def _():
        slots[1 + count] = slots[count]
        slots[1 + tiles + 1 + count] = slots[1 + tiles + count]


def attend(slots, queries, keys_ref, turned, partial, rotated, total, checks, *, tiles):
    devices, batches, tile_rows, width = queries.shape
    group = width // HEAD
    rows = tile_rows * group
    key_count = keys_ref.shape[0]
    pairs = (slots[0] + 1) // 2
    checks[...] = jnp.ones(checks.shape, jnp.float32)

    def tile_of(pair, side):
        tile = slots[1 + 2 * pair + side]
        return tile % devices, tile // devices

    def horizon_of(pair, side):
        return slots[2 + tiles + 2 * pair + side]

    def columns(pair):
        row = lax.broadcasted_iota(jnp.int32, (1, rows), 1) % tile_rows
        return jnp.concatenate([horizon_of(pair, side) + row for side in range(2)], axis=1)

    def scores(start, count):
        return (
            jnp.dot(
                keys_ref[pl.ds(start, count), :],
                rotated[...],
                preferred_element_type=jnp.float32,
            )
            * SCALE
        )

    def visible(start, count, limits):
        return (
            lax.broadcasted_iota(jnp.int32, (count, 2 * rows), 0) + start
            <= limits
        )

    def load(pair):
        for side in range(2):
            device, batch = tile_of(pair, side)
            tile = queries[device, batch]
            stacked = jnp.concatenate(
                [tile[:, part * HEAD : (part + 1) * HEAD] for part in range(group)], axis=0
            )
            rotated[:, side * rows : (side + 1) * rows] = stacked.T

    def run(start, count, limits):
        steps = count // KEYS
        offsets = [start + step * KEYS for step in range(steps)]
        ahead = [scores(offset, KEYS) for offset in offsets[:2]]
        added = None
        for step in range(steps):
            weights = jnp.exp2(ahead[step])
            if limits is not None:
                weights = jnp.where(visible(offsets[step], KEYS, limits), weights, 0.0)
            if step + 2 < steps:
                ahead.append(scores(offsets[step + 2], KEYS))
            new = jnp.dot(
                turned[:, pl.ds(offsets[step], KEYS)],
                weights.astype(jnp.bfloat16),
                preferred_element_type=jnp.float32,
            )
            added = new if added is None else added + new
        return added

    def finish(pair, summed, highest):
        mass = jnp.log2(summed) + highest
        high = mass.astype(jnp.bfloat16)
        middle = (mass - high.astype(jnp.float32)).astype(jnp.bfloat16)
        low = (mass - high.astype(jnp.float32) - middle.astype(jnp.float32)).astype(jnp.bfloat16)
        pad = lax.broadcasted_iota(jnp.int32, (PAD, 2 * rows), 0)
        terms = jnp.where(
            pad == 0,
            high.astype(jnp.float32),
            jnp.where(
                pad == 1,
                middle.astype(jnp.float32),
                jnp.where(pad == 2, low.astype(jnp.float32), 0.0),
            ),
        ).astype(jnp.bfloat16)
        blended = (total[:HEAD] * (1.0 / summed)).T.astype(jnp.bfloat16)
        for side in range(2):
            device, batch = tile_of(pair, side)
            part = slice(side * rows, (side + 1) * rows)
            partial[device, batch, :rows] = blended[part]
            partial[device, batch, rows:] = terms[:, part]

    def quick(pair, carry):
        load(pair)
        first = horizon_of(pair, 0)
        second = horizon_of(pair, 1)
        fewest = jnp.minimum(first, second)
        most = jnp.maximum(first, second)

        @pl.when(fewest == key_count)
        def _():
            total[...] = run(0, key_count, None)

        @pl.when(fewest < key_count)
        def _():
            limits = columns(pair)
            total[...] = jnp.zeros(total.shape, jnp.float32)
            full = (fewest + 1) // STEP
            last = jnp.minimum((most + tile_rows + STEP - 1) // STEP, key_count // STEP)

            def plain(step, carry):
                total[...] += run(pl.multiple_of(step * STEP, STEP), STEP, None)
                return carry

            def masked(step, carry):
                total[...] += run(pl.multiple_of(step * STEP, STEP), STEP, limits)
                return carry

            lax.fori_loop(0, full, plain, 0)
            lax.fori_loop(full, last, masked, 0)

        summed = total[HEAD : HEAD + 1, :]
        good = (summed > SMALL) & (summed < LARGE)
        checks[...] = jnp.minimum(checks[...], jnp.where(good, 1.0, 0.0))
        finish(pair, summed, 0.0)
        return carry

    lax.fori_loop(0, pairs, quick, 0)

    def exact(pair, carry):
        load(pair)
        limits = columns(pair)

        def measured(step):
            start = pl.multiple_of(step * KEYS, KEYS)
            return jnp.where(visible(start, KEYS, limits), scores(start, KEYS), -1e30)

        def highest_of(step, highest):
            return jnp.maximum(highest, jnp.max(measured(step), axis=0, keepdims=True))

        highest = lax.fori_loop(
            0, key_count // KEYS, highest_of, jnp.full((1, 2 * rows), -1e30, jnp.float32)
        )
        total[...] = jnp.zeros(total.shape, jnp.float32)

        def add(step, carry):
            weights = jnp.exp2(measured(step) - highest).astype(jnp.bfloat16)
            total[...] += jnp.dot(
                turned[:, pl.ds(pl.multiple_of(step * KEYS, KEYS), KEYS)],
                weights,
                preferred_element_type=jnp.float32,
            )
            return carry

        lax.fori_loop(0, key_count // KEYS, add, 0)
        finish(pair, total[HEAD : HEAD + 1, :], highest)
        return carry

    @pl.when(jnp.min(checks[...]) < 0.5)
    def _():
        lax.fori_loop(0, pairs, exact, 0)


def combine(me, tile_blocks, block_place, first, second, attended):
    devices, batches, padded, _ = first.shape
    top = tile_blocks.shape[1]
    rows = padded - PAD
    tile_rows = attended.shape[1]
    for batch in range(batches):
        owners = [
            block_place[tile_blocks[batch * devices + me[0], entry]] for entry in range(top)
        ]
        for half, returned in enumerate((first, second)):
            masses = []
            for owner in owners:
                terms = returned[owner, batch, rows:].astype(jnp.float32)
                masses.append(terms[0:1] + terms[1:2] + terms[2:3])
            highest = functools.reduce(jnp.maximum, masses)
            shares = [jnp.exp2(mass - highest) for mass in masses]
            inverse = 1.0 / functools.reduce(jnp.add, shares)
            stacked = jnp.concatenate([share * inverse for share in shares], axis=0)
            stacked = jnp.concatenate(
                [stacked, jnp.zeros((8 - top, rows), jnp.float32)], axis=0
            ).T
            blended = functools.reduce(
                jnp.add,
                [
                    stacked[:, entry : entry + 1] * returned[owner, batch, :rows].astype(jnp.float32)
                    for entry, owner in enumerate(owners)
                ],
            ).astype(jnp.bfloat16)
            for part in range(rows // tile_rows):
                column = (half * (rows // tile_rows) + part) * HEAD
                attended[batch, :, column : column + HEAD] = blended[
                    part * tile_rows : (part + 1) * tile_rows
                ]


def local(queries, keys, values, tile_blocks, block_place, tile_offset):
    devices = lax.axis_size("seq")
    batches, _, tile_rows, features = queries.shape
    _, key_count, key_features = keys.shape
    shared = key_features // HEAD
    width = features // shared
    rows = tile_rows * (width // HEAD)
    tiles = tile_blocks.shape[0]
    me = lax.axis_index("seq").astype(jnp.int32)[None]
    smem = pl.BlockSpec(memory_space=pltpu.SMEM)
    vmem = pl.BlockSpec(memory_space=pltpu.VMEM)
    turned, slots = pl.pallas_call(
        functools.partial(prepare, tile_rows=tile_rows),
        out_shape=(
            jax.ShapeDtypeStruct((shared, HEAD + PAD, key_count), jnp.bfloat16),
            jax.ShapeDtypeStruct((2 * tiles + 4,), jnp.int32),
        ),
        in_specs=[smem, smem, smem, smem, vmem],
        out_specs=(vmem, smem),
        name="prepare",
    )(me, tile_blocks, block_place, tile_offset, values[0])
    arrived = []
    for head in range(shared):
        tile = queries[:, 0, :, head * width : (head + 1) * width]
        outgoing = jnp.broadcast_to(tile[None], (devices,) + tile.shape)
        arrived.append(
            lax.all_to_all(outgoing, "seq", split_axis=0, concat_axis=0, tiled=True)
        )
    returned = []
    for head in range(shared):
        partial = pl.pallas_call(
            functools.partial(attend, tiles=tiles),
            grid=(1,),
            out_shape=jax.ShapeDtypeStruct(
                (devices, batches, rows + PAD, HEAD), jnp.bfloat16
            ),
            in_specs=[
                smem,
                vmem,
                pl.BlockSpec((None, key_count, HEAD), lambda i, head=head: (0, 0, head)),
                pl.BlockSpec((None, HEAD + PAD, key_count), lambda i, head=head: (head, 0, 0)),
            ],
            out_specs=vmem,
            scratch_shapes=[
                pltpu.VMEM((HEAD, 2 * rows), jnp.bfloat16),
                pltpu.VMEM((HEAD + PAD, 2 * rows), jnp.float32),
                pltpu.VMEM((1, 2 * rows), jnp.float32),
            ],
            name="attend",
        )(slots, arrived[head], keys, turned)
        returned.append(
            lax.all_to_all(partial, "seq", split_axis=0, concat_axis=0, tiled=True)
        )
    out = pl.pallas_call(
        combine,
        out_shape=jax.ShapeDtypeStruct((batches, tile_rows, features), jnp.bfloat16),
        in_specs=[smem, smem, smem, vmem, vmem],
        out_specs=vmem,
        name="combine",
    )(me, tile_blocks, block_place, *returned)
    return out[:, None]


def solution(mesh):
    placed = (
        P(None, ("groups", "seq"), None, "heads"),
        P(("groups", "seq"), None, "heads"),
        P(("groups", "seq"), None, "heads"),
        P("groups", None),
        P("groups"),
        P("groups"),
    )
    return jax.shard_map(
        local,
        mesh=mesh,
        in_specs=placed,
        out_specs=P(None, ("groups", "seq"), None, "heads"),
        check_vma=False,
    )
```

time: 311 us -> 245 us (0.79); the launches traced: 308 us -> 247 us
  blocking collectives: 0 us -> 112 us
  local copies, waits for them, and re-layouts: 96.9 us -> 2.5 us
  Pallas kernels: 0 us -> 53.5 us
  waiting for transfers between devices: 39.6 us -> 0.01 us
  other arithmetic: 28.6 us -> 0 us
  starting transfers between devices: 106 us -> 79.1 us
  matrix products: 24.8 us -> 0 us
  loops' own time: 11.5 us -> 0 us
    all_to_all x0 -> x2, blocking collectives: none -> 112 us  [the longest x1 90.7 us: local(): lax.all_to_all(partial, 'seq', split_axis=0, concat_axis=0, tiled=True)]
    pallas_call x0 -> x4, Pallas kernels: none -> 53.5 us  [the longest x2 47 us: local(): pl.pallas_call(functools.partial(attend, tiles=tiles), grid=(1,), out_sha...]
    all_to_all x6 -> x2, waiting for transfers between devices: 39.6 us -> 0.01 us  [the longest x1 0.01 us: local(): lax.all_to_all(partial, 'seq', split_axis=0, concat_axis=0, tiled=True)]
    all_to_all x6 -> x2, starting transfers between devices: 106 us -> 79.1 us  [the longest x1 75.5 us: local(): lax.all_to_all(partial, 'seq', split_axis=0, concat_axis=0, tiled=True)]
    dot_general x22 -> x0, matrix products: 24.8 us -> none  [the longest x10 17.5 us: attend(): jnp.einsum('rgh,kh->grk', tile_query, key_head, preferred_element_type=jn...]
    dynamic_slice x26 -> x0, local copies, waits for them, and re-layouts: 20.1 us -> none  [the longest x16 20 us: local(): lax.map(one_slot, (arrived, horizons, slot_live))]
    dynamic_update_slice x48 -> x0, local copies, waits for them, and re-layouts: 17.7 us -> none  [local(): lax.map(one_slot, (arrived, horizons, slot_live))]
    unnamed x26 -> x7, local copies, waits for them, and re-layouts: 16.5 us -> 0.69 us
  transfers between devices with their start and end apart: 6 -> 2, of which waited for: 3 -> 0; matrix products, arithmetic and copies ran while one was open for 47% -> 0% of each run, Pallas kernels for 0% -> 21%
where the time goes in v1:
time: 245 us; the launch traced here: 247 us
  blocking collectives  112 us (46%)
  starting transfers between devices  79.1 us (32%)
  Pallas kernels  53.5 us (22%)
  local copies, waits for them, and re-layouts  2.5 us (1%)
    all_to_all x1, blocking collectives, local(): lax.all_to_all(partial, 'seq', split_axis=0, concat_axis=0, tiled=True)  90.7 us
    all_to_all x1, starting transfers between devices, local(): lax.all_to_all(partial, 'seq', split_axis=0, concat_axis=0, tiled=True)  75.5 us
    pallas_call x2, Pallas kernels, local(): pl.pallas_call(functools.partial(attend, tiles=tiles), grid=(1,), out_sha...  47 us
    all_to_all x1, blocking collectives, local(): lax.all_to_all(outgoing, 'seq', split_axis=0, concat_axis=0, tiled=True)  21.7 us
  transfers between devices with their start and end apart: 2, of which 0 were waited for; matrix products, arithmetic and copies ran while one was open for 0% of the time, Pallas kernels for 21%

profile of v1, /device:TPU:0, one launch (start us, length us, event | category | flops | bytes accessed | tf_op | source)
XLA Modules:
  0.0 247.5 jit_solution(3945161207982279772)
XLA Ops:
  0.0 0.0 copy-start.2
  0.0 0.9 slice_bitcast_fusion
  0.9 0.1 broadcast_in_dim.22
  1.0 21.7 %all_to_all.20.queries = bf16[8,2,16,1024]{3,2,1,0:T(8,128)(2,1)} all-to-all(bf16[8,2,16,1024]{3,2,1,0:T(8,128)(2,1)S(1)} %broadcast_in_dim.22), channel_id=1, replica_groups=mesh['groups'=2,'seq'=8,'heads'=2] {'seq'}, dimensions={0} | all-to-all | bytes 1048576 | tf_op jit(solution)/shard_map/all_to_all | solution.py:277
  22.7 0.9 broadcast_in_dim.24
  23.5 3.6 %all-to-all-start.2 = ((bf16[8,2,16,1024]{3,2,1,0:T(8,128)(2,1)}), bf16[8,2,16,1024]{3,2,1,0:T(8,128)(2,1)S(1)}, u32[]{:S(2)}, u32[]{:S(2)}) async-start(bf16[8,2,16,1024]{3,2,1,0:T(8,128)(2,1)} %broadcast_in_dim.24), calls=%async_computation.2 | async-start | bytes 1048576 | tf_op jit(solution)/shard_map/all_to_all | solution.py:277
  27.1 0.0 copy-done.2
  27.1 0.7 copy.8.tile_blocks
  27.8 4.0 %prepare.1 = (bf16[2,144,4096]{2,1,0:T(8,128)(2,1)}, s32[36]{0:T(128)}) custom-call(s32[1]{0:T(128)} %bitcast.me, s32[16,4]{1,0:T(8,128)} %copy.8.tile_blocks, s32[8]{0:T(128)} %block_place.3, s32[16]{0:T(128)} %tile_offset.1, bf16[4096,256]{1,0:T(8,128)(2,1)} %bitcast.9), custom_call_target="tpu_custom_call" | custom-call | tf_op jit(solution)/shard_map/prepare/pallas_call | solution.py:262
  31.8 23.5 %attend.2 = bf16[8,2,144,128]{3,2,1,0:T(8,128)(2,1)} custom-call(s32[36]{0:T(128)} %get-tuple-element.7.slots, bf16[8,2,16,1024]{3,2,1,0:T(8,128)(2,1)} %all_to_all.20.queries, bf16[1,4096,256]{2,1,0:T(8,128)(2,1)} %keys_ref.3, bf16[2,144,4096]{2,1,0:T(8,128)(2,1)} %get-tuple-element.8.turned), custom_call_target="tpu_custom_call" | custom-call | tf_op jit(solution)/shard_map/attend/pallas_call | solution.py:281
  55.3 0.0 all-to-all-done.2.queries
  55.3 0.0 copy-start.1
  55.3 75.5 %all-to-all-start.1 = ((bf16[8,2,144,128]{3,2,1,0:T(8,128)(2,1)}), bf16[8,2,144,128]{3,2,1,0:T(8,128)(2,1)S(1)}, u32[]{:S(2)}, u32[]{:S(2)}) async-start(bf16[8,2,144,128]{3,2,1,0:T(8,128)(2,1)} %attend.2), calls=%async_computation.1 | async-start | bytes 1179648 | tf_op jit(solution)/shard_map/all_to_all | solution.py:302
  130.8 0.0 copy-done.1
  130.8 23.5 %attend.3 = bf16[8,2,144,128]{3,2,1,0:T(8,128)(2,1)} custom-call(s32[36]{0:T(128)} %get-tuple-element.7.slots, bf16[8,2,16,1024]{3,2,1,0:T(8,128)(2,1)} %copy-done.1, bf16[1,4096,256]{2,1,0:T(8,128)(2,1)} %keys_ref.3, bf16[2,144,4096]{2,1,0:T(8,128)(2,1)} %get-tuple-element.8.turned), custom_call_target="tpu_custom_call" | custom-call | tf_op jit(solution)/shard_map/attend/pallas_call | solution.py:281
  154.3 0.0 all-to-all-done.1.first
  154.3 0.0 copy-start
  154.3 90.7 %all_to_all.21.second = bf16[8,2,144,128]{3,2,1,0:T(8,128)(2,1)} all-to-all(bf16[8,2,144,128]{3,2,1,0:T(8,128)(2,1)} %attend.3), channel_id=1, replica_groups=mesh['groups'=2,'seq'=8,'heads'=2] {'seq'}, dimensions={0} | all-to-all | bytes 1179648 | tf_op jit(solution)/shard_map/all_to_all | solution.py:302
  245.0 0.0 copy-done
  245.0 2.5 %combine.1 = bf16[2,16,2048]{2,1,0:T(8,128)(2,1)} custom-call(s32[1]{0:T(128)} %bitcast.me, s32[16,4]{1,0:T(8,128)} %copy.8.tile_blocks, s32[8]{0:T(128)} %block_place.3, bf16[8,2,144,128]{3,2,1,0:T(8,128)(2,1)} %copy-done, bf16[8,2,144,128]{3,2,1,0:T(8,128)(2,1)} %all_to_all.21.second), custom_call_target="tpu_custom_call" | custom-call | tf_op jit(solution)/shard_map/combine/pallas_call | solution.py:304
Async XLA Ops:
  0.0 27.1 %copy-start.2 = (s32[16,4]{0,1:T(4,128)S(1)}, s32[16,4]{0,1:T(4,128)}, u32[]{:S(2)}) copy-start(s32[16,4]{0,1:T(4,128)} %param.9) | copy-start | bytes 772
  23.5 31.7 %all-to-all-start.2 = ((bf16[8,2,16,1024]{3,2,1,0:T(8,128)(2,1)}), bf16[8,2,16,1024]{3,2,1,0:T(8,128)(2,1)S(1)}, u32[]{:S(2)}, u32[]{:S(2)}) async-start(bf16[8,2,16,1024]{3,2,1,0:T(8,128)(2,1)} %broadcast_in_dim.24), calls=%async_computation.2 | async-start | bytes 1048576 | tf_op jit(solution)/shard_map/all_to_all | solution.py:277
  55.3 75.5 %copy-start.1 = (bf16[8,2,16,1024]{3,2,1,0:T(8,128)(2,1)}, bf16[8,2,16,1024]{3,2,1,0:T(8,128)(2,1)S(1)}, u32[]{:S(2)}) copy-start(bf16[8,2,16,1024]{3,2,1,0:T(8,128)(2,1)S(1)} %all-to-all-done.2.queries) | copy-start | bytes 1572868
  55.3 99.0 %all-to-all-start.1 = ((bf16[8,2,144,128]{3,2,1,0:T(8,128)(2,1)}), bf16[8,2,144,128]{3,2,1,0:T(8,128)(2,1)S(1)}, u32[]{:S(2)}, u32[]{:S(2)}) async-start(bf16[8,2,144,128]{3,2,1,0:T(8,128)(2,1)} %attend.2), calls=%async_computation.1 | async-start | bytes 1179648 | tf_op jit(solution)/shard_map/all_to_all | solution.py:302
  154.3 90.7 %copy-start = (bf16[8,2,144,128]{3,2,1,0:T(8,128)(2,1)}, bf16[8,2,144,128]{3,2,1,0:T(8,128)(2,1)S(1)}, u32[]{:S(2)}) copy-start(bf16[8,2,144,128]{3,2,1,0:T(8,128)(2,1)S(1)} %all-to-all-done.1.first) | copy-start | bytes 1769476

commit v2 on v1

--- a/solution.py
+++ b/solution.py
@@ -10,7 +10,6 @@
 HEAD = 128
 SCALE = HEAD ** (-0.5) * 1.4426950408889634
 KEYS = 256
-STEP = 512
 SMALL = 2.0**-60
 LARGE = 2.0**100
 PAD = 16
@@ -34,27 +33,29 @@
 
     mine = lax.fori_loop(0, block_count, find, 0)
 
-    def visit(tile, count):
+    def visit(tile, counts, late):
+        count = counts
         entries = [tile_blocks[tile, entry] for entry in range(top)]
-        own = functools.reduce(jnp.maximum, entries)
+        own = functools.reduce(jnp.maximum, entries) == mine
         named = functools.reduce(jnp.logical_or, [entry == mine for entry in entries])
-
-        @pl.when(named)
+        chosen = named & (own if late else jnp.logical_not(own))
+
+        @pl.when(chosen)
         def _():
-            slots[1 + count] = tile
-            slots[1 + tiles + 1 + count] = jnp.where(
-                own == mine, tile_offset[tile] * tile_rows, keys
-            )
-
-        return count + named.astype(jnp.int32)
-
-    count = lax.fori_loop(0, tiles, visit, 0)
-    slots[0] = count
+            slots[2 + count] = tile
+            slots[3 + tiles + count] = tile_offset[tile] * tile_rows if late else keys
+
+        return count + chosen.astype(jnp.int32)
+
+    whole = lax.fori_loop(0, tiles, functools.partial(visit, late=False), 0)
+    count = lax.fori_loop(0, tiles, functools.partial(visit, late=True), whole)
+    slots[0] = whole // 2
+    slots[1] = (count + 1) // 2
 
     @pl.when(count % 2 == 1)
     def _():
-        slots[1 + count] = slots[count]
-        slots[1 + tiles + 1 + count] = slots[1 + tiles + count]
+        slots[2 + count] = slots[1 + count]
+        slots[3 + tiles + count] = slots[2 + tiles + count]
 
 
 def attend(slots, queries, keys_ref, turned, partial, rotated, total, checks, *, tiles):
@@ -62,70 +63,39 @@
     group = width // HEAD
     rows = tile_rows * group
     key_count = keys_ref.shape[0]
-    pairs = (slots[0] + 1) // 2
+    columns = 2 * rows
+    steps = key_count // (2 * KEYS)
     checks[...] = jnp.ones(checks.shape, jnp.float32)
+    rotated[...] = jnp.zeros(rotated.shape, rotated.dtype)
 
     def tile_of(pair, side):
-        tile = slots[1 + 2 * pair + side]
+        tile = slots[2 + 2 * pair + side]
         return tile % devices, tile // devices
 
-    def horizon_of(pair, side):
-        return slots[2 + tiles + 2 * pair + side]
-
-    def columns(pair):
+    def limits_of(pair):
         row = lax.broadcasted_iota(jnp.int32, (1, rows), 1) % tile_rows
-        return jnp.concatenate([horizon_of(pair, side) + row for side in range(2)], axis=1)
-
-    def scores(start, count):
-        return (
-            jnp.dot(
-                keys_ref[pl.ds(start, count), :],
-                rotated[...],
-                preferred_element_type=jnp.float32,
-            )
-            * SCALE
+        return jnp.concatenate(
+            [slots[3 + tiles + 2 * pair + side] + row for side in range(2)], axis=1
         )
 
-    def visible(start, count, limits):
-        return (
-            lax.broadcasted_iota(jnp.int32, (count, 2 * rows), 0) + start
-            <= limits
-        )
-
-    def load(pair):
+    def visible(start, limits):
+        return lax.broadcasted_iota(jnp.int32, (KEYS, columns), 0) <= limits - start
+
+    def load(pair, place):
         for side in range(2):
             device, batch = tile_of(pair, side)
             tile = queries[device, batch]
             stacked = jnp.concatenate(
                 [tile[:, part * HEAD : (part + 1) * HEAD] for part in range(group)], axis=0
             )
-            rotated[:, side * rows : (side + 1) * rows] = stacked.T
-
-    def run(start, count, limits):
-        steps = count // KEYS
-        offsets = [start + step * KEYS for step in range(steps)]
-        ahead = [scores(offset, KEYS) for offset in offsets[:2]]
-        added = None
-        for step in range(steps):
-            weights = jnp.exp2(ahead[step])
-            if limits is not None:
-                weights = jnp.where(visible(offsets[step], KEYS, limits), weights, 0.0)
-            if step + 2 < steps:
-                ahead.append(scores(offsets[step + 2], KEYS))
-            new = jnp.dot(
-                turned[:, pl.ds(offsets[step], KEYS)],
-                weights.astype(jnp.bfloat16),
-                preferred_element_type=jnp.float32,
-            )
-            added = new if added is None else added + new
-        return added
+            rotated[place, :HEAD, side * rows : (side + 1) * rows] = stacked.T
 
     def finish(pair, summed, highest):
         mass = jnp.log2(summed) + highest
         high = mass.astype(jnp.bfloat16)
         middle = (mass - high.astype(jnp.float32)).astype(jnp.bfloat16)
         low = (mass - high.astype(jnp.float32) - middle.astype(jnp.float32)).astype(jnp.bfloat16)
-        pad = lax.broadcasted_iota(jnp.int32, (PAD, 2 * rows), 0)
+        pad = lax.broadcasted_iota(jnp.int32, (PAD, columns), 0)
         terms = jnp.where(
             pad == 0,
             high.astype(jnp.float32),
@@ -142,75 +112,112 @@
             partial[device, batch, :rows] = blended[part]
             partial[device, batch, rows:] = terms[:, part]
 
-    def quick(pair, carry):
-        load(pair)
-        first = horizon_of(pair, 0)
-        second = horizon_of(pair, 1)
-        fewest = jnp.minimum(first, second)
-        most = jnp.maximum(first, second)
-
-        @pl.when(fewest == key_count)
-        def _():
-            total[...] = run(0, key_count, None)
-
-        @pl.when(fewest < key_count)
-        def _():
-            limits = columns(pair)
-            total[...] = jnp.zeros(total.shape, jnp.float32)
-            full = (fewest + 1) // STEP
-            last = jnp.minimum((most + tile_rows + STEP - 1) // STEP, key_count // STEP)
-
-            def plain(step, carry):
-                total[...] += run(pl.multiple_of(step * STEP, STEP), STEP, None)
-                return carry
-
-            def masked(step, carry):
-                total[...] += run(pl.multiple_of(step * STEP, STEP), STEP, limits)
-                return carry
-
-            lax.fori_loop(0, full, plain, 0)
-            lax.fori_loop(full, last, masked, 0)
-
-        summed = total[HEAD : HEAD + 1, :]
-        good = (summed > SMALL) & (summed < LARGE)
-        checks[...] = jnp.minimum(checks[...], jnp.where(good, 1.0, 0.0))
-        finish(pair, summed, 0.0)
-        return carry
-
-    lax.fori_loop(0, pairs, quick, 0)
-
-    def exact(pair, carry):
-        load(pair)
-        limits = columns(pair)
+    def quick(first, last, masked, accumulators):
+        score = accumulators[:2], accumulators[2:4]
+        value = accumulators[4:]
+
+        def score_step(unit, place, step):
+            start = (2 * step + unit) * KEYS
+            block = keys_ref[start : start + KEYS]
+            pltpu.matmul_push_rhs(rotated[place], 0, unit)
+            pltpu.matmul_acc_lhs(
+                score[unit][step % 2], jnp.concatenate([block, block], axis=1), 0
+            )
+
+        def value_step(unit, step, limits):
+            start = (2 * step + unit) * KEYS
+            weights = jnp.exp2(pltpu.matmul_pop(score[unit][step % 2]) * SCALE)
+            if masked:
+                weights = jnp.where(visible(start, limits), weights, 0.0)
+            pltpu.matmul_push_rhs(weights.astype(jnp.bfloat16), 1, unit)
+            pltpu.matmul_acc_lhs(value[unit], turned[:, start : start + KEYS], 1)
+
+        def close(pair, real):
+            total[...] = pltpu.matmul_pop(value[0]) + pltpu.matmul_pop(value[1])
+            summed = total[HEAD : HEAD + 1, :]
+            good = (summed > SMALL) & (summed < LARGE)
+            checks[...] = jnp.minimum(checks[...], jnp.where(good | jnp.logical_not(real), 1.0, 0.0))
+            finish(pair, summed, 0.0)
+
+        for unit in range(2):
+            for accumulator in score[unit] + value[unit : unit + 1]:
+                pltpu.matmul_pop(accumulator)
+        load(first, first % 2)
+        for unit in range(2):
+            score_step(unit, first % 2, 0)
+
+        def body(pair, carry):
+            place = pair % 2
+            limits = limits_of(pair) if masked else None
+            close(jnp.maximum(pair - 1, first), pair > first)
+            load(jnp.minimum(pair + 1, last - 1), 1 - place)
+            for step in range(steps):
+                for unit in range(2):
+                    if step + 1 < steps:
+                        score_step(unit, place, step + 1)
+                    else:
+                        score_step(unit, 1 - place, 0)
+                    value_step(unit, step, limits)
+            return carry
+
+        lax.fori_loop(first, last, body, 0)
+        for unit in range(2):
+            pltpu.matmul_pop(score[unit][0])
+        close(last - 1, True)
+
+    def exact(pair, carry, accumulators):
+        score, value = accumulators[0], accumulators[4]
+        load(pair, 0)
+        limits = limits_of(pair)
 
         def measured(step):
             start = pl.multiple_of(step * KEYS, KEYS)
-            return jnp.where(visible(start, KEYS, limits), scores(start, KEYS), -1e30)
+            block = keys_ref[pl.ds(start, KEYS), :]
+            pltpu.matmul_push_rhs(rotated[0], 0, 0)
+            pltpu.matmul_acc_lhs(score, jnp.concatenate([block, block], axis=1), 0)
+            scores = pltpu.matmul_pop(score) * SCALE
+            return jnp.where(visible(start, limits), scores, -1e30)
 
         def highest_of(step, highest):
             return jnp.maximum(highest, jnp.max(measured(step), axis=0, keepdims=True))
 
         highest = lax.fori_loop(
-            0, key_count // KEYS, highest_of, jnp.full((1, 2 * rows), -1e30, jnp.float32)
+            0, key_count // KEYS, highest_of, jnp.full((1, columns), -1e30, jnp.float32)
         )
-        total[...] = jnp.zeros(total.shape, jnp.float32)
 
         def add(step, carry):
             weights = jnp.exp2(measured(step) - highest).astype(jnp.bfloat16)
-            total[...] += jnp.dot(
-                turned[:, pl.ds(pl.multiple_of(step * KEYS, KEYS), KEYS)],
-                weights,
-                preferred_element_type=jnp.float32,
+            pltpu.matmul_push_rhs(weights, 1, 0)
+            pltpu.matmul_acc_lhs(
+                value, turned[:, pl.ds(pl.multiple_of(step * KEYS, KEYS), KEYS)], 1
             )
             return carry
 
         lax.fori_loop(0, key_count // KEYS, add, 0)
+        total[...] = pltpu.matmul_pop(value)
         finish(pair, total[HEAD : HEAD + 1, :], highest)
         return carry
 
-    @pl.when(jnp.min(checks[...]) < 0.5)
-    def _():
-        lax.fori_loop(0, pairs, exact, 0)
+    def every(*accumulators):
+        @pl.when(slots[0] > 0)
+        def _():
+            quick(0, slots[0], False, accumulators)
+
+        @pl.when(slots[1] > slots[0])
+        def _():
+            quick(slots[0], slots[1], True, accumulators)
+
+        @pl.when(jnp.min(checks[...]) < 0.5)
+        def _():
+            lax.fori_loop(
+                0, slots[1], functools.partial(exact, accumulators=accumulators), 0
+            )
+
+    pl.run_scoped(
+        every,
+        *[pltpu.ACC(unit)((KEYS, columns), jnp.float32) for unit in (0, 0, 1, 1)],
+        *[pltpu.ACC(unit)((HEAD + PAD, columns), jnp.float32) for unit in (0, 1)],
+    )
 
 
 def combine(me, tile_blocks, block_place, first, second, attended):
@@ -263,10 +270,11 @@
         functools.partial(prepare, tile_rows=tile_rows),
         out_shape=(
             jax.ShapeDtypeStruct((shared, HEAD + PAD, key_count), jnp.bfloat16),
-            jax.ShapeDtypeStruct((2 * tiles + 4,), jnp.int32),
+            jax.ShapeDtypeStruct((2 * tiles + 5,), jnp.int32),
         ),
         in_specs=[smem, smem, smem, smem, vmem],
         out_specs=(vmem, smem),
+        cost_estimate=pl.CostEstimate(flops=10**10, transcendentals=0, bytes_accessed=2**22),
         name="prepare",
     )(me, tile_blocks, block_place, tile_offset, values[0])
     arrived = []
@@ -292,10 +300,11 @@
             ],
             out_specs=vmem,
             scratch_shapes=[
-                pltpu.VMEM((HEAD, 2 * rows), jnp.bfloat16),
+                pltpu.VMEM((2, 2 * HEAD, 2 * rows), jnp.bfloat16),
                 pltpu.VMEM((HEAD + PAD, 2 * rows), jnp.float32),
                 pltpu.VMEM((1, 2 * rows), jnp.float32),
             ],
+            cost_estimate=pl.CostEstimate(flops=10**10, transcendentals=0, bytes_accessed=2**22),
             name="attend",
         )(slots, arrived[head], keys, turned)
         returned.append(

time: 245 us -> 212 us (0.87); the launches traced: 247 us -> 211 us
  blocking collectives: 112 us -> 38.3 us
  Pallas kernels: 53.5 us -> 126 us
  starting transfers between devices: 79.1 us -> 33.6 us
  waiting for transfers between devices: 0.01 us -> 8.9 us
    pallas_call x2, Pallas kernels: 47 us -> 120 us  [local(): pl.pallas_call(functools.partial(attend, tiles=tiles), grid=(1,), out_sha...]
    all_to_all x1, starting transfers between devices: 75.5 us -> 22.6 us  [local(): lax.all_to_all(partial, 'seq', split_axis=0, concat_axis=0, tiled=True)]
    all_to_all x1, blocking collectives: 90.7 us -> 38.3 us  [local(): lax.all_to_all(partial, 'seq', split_axis=0, concat_axis=0, tiled=True)]
    all_to_all x1 -> x0, blocking collectives: 21.7 us -> none  [local(): lax.all_to_all(outgoing, 'seq', split_axis=0, concat_axis=0, tiled=True)]
    all_to_all x1 -> x2, waiting for transfers between devices: 0.01 us -> 8.9 us  [local(): lax.all_to_all(outgoing, 'seq', split_axis=0, concat_axis=0, tiled=True)]
    all_to_all x1 -> x2, starting transfers between devices: 3.59 us -> 10.9 us  [local(): lax.all_to_all(outgoing, 'seq', split_axis=0, concat_axis=0, tiled=True)]
  transfers between devices with their start and end apart: 2 -> 3, of which waited for: 0 -> 1; matrix products, arithmetic and copies ran while one was open for 0% -> 1% of each run, Pallas kernels for 21% -> 59%
where the time goes in v2:
time: 212 us; the launch traced here: 211 us
  Pallas kernels  126 us (59%)
  blocking collectives  38.3 us (18%)
  starting transfers between devices  33.6 us (16%)
  waiting for transfers between devices  8.9 us (4%)
  local copies, waits for them, and re-layouts  4.04 us (2%)
    pallas_call x2, Pallas kernels, local(): pl.pallas_call(functools.partial(attend, tiles=tiles), grid=(1,), out_sha...  120 us
    all_to_all x1, blocking collectives, local(): lax.all_to_all(partial, 'seq', split_axis=0, concat_axis=0, tiled=True)  38.3 us
    all_to_all x1, starting transfers between devices, local(): lax.all_to_all(partial, 'seq', split_axis=0, concat_axis=0, tiled=True)  22.6 us
    all_to_all x2, starting transfers between devices, local(): lax.all_to_all(outgoing, 'seq', split_axis=0, concat_axis=0, tiled=True)  10.9 us
    all_to_all x2, waiting for transfers between devices, local(): lax.all_to_all(outgoing, 'seq', split_axis=0, concat_axis=0, tiled=True)  8.9 us
  transfers between devices with their start and end apart: 3, of which 1 were waited for; matrix products, arithmetic and copies ran while one was open for 1% of the time, Pallas kernels for 59%

profile of v2, /device:TPU:0, one launch (start us, length us, event | category | flops | bytes accessed | tf_op | source)
XLA Modules:
  0.0 211.3 jit_solution(7872303135646381537)
XLA Ops:
  0.0 0.9 slice_bitcast_fusion
  0.9 0.9 broadcast_in_dim.22
  1.8 7.3 %all-to-all-start = ((bf16[8,2,16,1024]{3,2,1,0:T(8,128)(2,1)}), bf16[8,2,16,1024]{3,2,1,0:T(8,128)(2,1)S(1)}, u32[]{:S(2)}, u32[]{:S(2)}) async-start(bf16[8,2,16,1024]{3,2,1,0:T(8,128)(2,1)} %broadcast_in_dim.22), calls=%async_computation | async-start | bytes 1048576 | tf_op jit(solution)/shard_map/all_to_all | solution.py:285
  9.0 1.3 copy.8.tile_blocks
  10.4 4.2 %prepare.1 = (bf16[2,144,4096]{2,1,0:T(8,128)(2,1)}, s32[37]{0:T(128)}) custom-call(s32[1]{0:T(128)} %bitcast.me, s32[16,4]{1,0:T(8,128)} %copy.8.tile_blocks, s32[8]{0:T(128)} %block_place.3, s32[16]{0:T(128)} %tile_offset.1, bf16[4096,256]{1,0:T(8,128)(2,1)} %bitcast.9), custom_call_target="tpu_custom_call" | custom-call | flops 10000000000 | bytes 4194304 | tf_op jit(solution)/shard_map/prepare/pallas_call | solution.py:269
  14.6 8.9 %all-to-all-done.queries = bf16[8,2,16,1024]{3,2,1,0:T(8,128)(2,1)S(1)} async-done(((bf16[8,2,16,1024]{3,2,1,0:T(8,128)(2,1)}), bf16[8,2,16,1024]{3,2,1,0:T(8,128)(2,1)S(1)}, u32[]{:S(2)}, u32[]{:S(2)}) %all-to-all-start) | async-done | bytes 524320 | tf_op jit(solution)/shard_map/all_to_all | solution.py:285
  23.5 0.0 copy-start.1
  23.5 0.9 broadcast_in_dim.24
  24.5 3.6 %all-to-all-start.2 = ((bf16[8,2,16,1024]{3,2,1,0:T(8,128)(2,1)}), bf16[8,2,16,1024]{3,2,1,0:T(8,128)(2,1)S(1)}, u32[]{:S(2)}, u32[]{:S(2)}) async-start(bf16[8,2,16,1024]{3,2,1,0:T(8,128)(2,1)} %broadcast_in_dim.24), calls=%async_computation.2 | async-start | bytes 1048576 | tf_op jit(solution)/shard_map/all_to_all | solution.py:285
  28.1 0.0 copy-done.1
  28.1 59.9 %attend.2 = bf16[8,2,144,128]{3,2,1,0:T(8,128)(2,1)} custom-call(s32[37]{0:T(128)} %get-tuple-element.7.slots, bf16[8,2,16,1024]{3,2,1,0:T(8,128)(2,1)} %copy-done.1, bf16[1,4096,256]{2,1,0:T(8,128)(2,1)} %keys_ref.3, bf16[2,144,4096]{2,1,0:T(8,128)(2,1)} %get-tuple-element.8.turned), custom_call_target="tpu_custom_call" | custom-call | flops 10000000000 | bytes 4194304 | tf_op jit(solution)/shard_map/attend/pallas_call | solution.py:289
  88.0 0.0 all-to-all-done.2.queries
  88.0 0.0 copy-start.2
  88.0 22.6 %all-to-all-start.1 = ((bf16[8,2,144,128]{3,2,1,0:T(8,128)(2,1)}), bf16[8,2,144,128]{3,2,1,0:T(8,128)(2,1)S(1)}, u32[]{:S(2)}, u32[]{:S(2)}) async-start(bf16[8,2,144,128]{3,2,1,0:T(8,128)(2,1)} %attend.2), calls=%async_computation.1 | async-start | bytes 1179648 | tf_op jit(solution)/shard_map/all_to_all | solution.py:311
  110.6 0.0 copy-done.2
  110.6 59.8 %attend.3 = bf16[8,2,144,128]{3,2,1,0:T(8,128)(2,1)} custom-call(s32[37]{0:T(128)} %get-tuple-element.7.slots, bf16[8,2,16,1024]{3,2,1,0:T(8,128)(2,1)} %copy-done.2, bf16[1,4096,256]{2,1,0:T(8,128)(2,1)} %keys_ref.3, bf16[2,144,4096]{2,1,0:T(8,128)(2,1)} %get-tuple-element.8.turned), custom_call_target="tpu_custom_call" | custom-call | flops 10000000000 | bytes 4194304 | tf_op jit(solution)/shard_map/attend/pallas_call | solution.py:289
  170.4 0.0 all-to-all-done.1.first
  170.4 0.0 copy-start
  170.4 38.3 %all_to_all.20.second = bf16[8,2,144,128]{3,2,1,0:T(8,128)(2,1)} all-to-all(bf16[8,2,144,128]{3,2,1,0:T(8,128)(2,1)} %attend.3), channel_id=1, replica_groups=mesh['groups'=2,'seq'=8,'heads'=2] {'seq'}, dimensions={0} | all-to-all | bytes 1179648 | tf_op jit(solution)/shard_map/all_to_all | solution.py:311
  208.8 0.0 copy-done
  208.8 2.5 %combine.1 = bf16[2,16,2048]{2,1,0:T(8,128)(2,1)} custom-call(s32[1]{0:T(128)} %bitcast.me, s32[16,4]{1,0:T(8,128)} %copy.8.tile_blocks, s32[8]{0:T(128)} %block_place.3, bf16[8,2,144,128]{3,2,1,0:T(8,128)(2,1)} %copy-done, bf16[8,2,144,128]{3,2,1,0:T(8,128)(2,1)} %all_to_all.20.second), custom_call_target="tpu_custom_call" | custom-call | tf_op jit(solution)/shard_map/combine/pallas_call | solution.py:313
Async XLA Ops:
  1.8 21.8 %all-to-all-start = ((bf16[8,2,16,1024]{3,2,1,0:T(8,128)(2,1)}), bf16[8,2,16,1024]{3,2,1,0:T(8,128)(2,1)S(1)}, u32[]{:S(2)}, u32[]{:S(2)}) async-start(bf16[8,2,16,1024]{3,2,1,0:T(8,128)(2,1)} %broadcast_in_dim.22), calls=%async_computation | async-start | bytes 1048576 | tf_op jit(solution)/shard_map/all_to_all | solution.py:285
  23.5 4.6 %copy-start.1 = (bf16[8,2,16,1024]{3,2,1,0:T(8,128)(2,1)}, bf16[8,2,16,1024]{3,2,1,0:T(8,128)(2,1)S(1)}, u32[]{:S(2)}) copy-start(bf16[8,2,16,1024]{3,2,1,0:T(8,128)(2,1)S(1)} %all-to-all-done.queries) | copy-start | bytes 1572868
  24.5 63.5 %all-to-all-start.2 = ((bf16[8,2,16,1024]{3,2,1,0:T(8,128)(2,1)}), bf16[8,2,16,1024]{3,2,1,0:T(8,128)(2,1)S(1)}, u32[]{:S(2)}, u32[]{:S(2)}) async-start(bf16[8,2,16,1024]{3,2,1,0:T(8,128)(2,1)} %broadcast_in_dim.24), calls=%async_computation.2 | async-start | bytes 1048576 | tf_op jit(solution)/shard_map/all_to_all | solution.py:285
  88.0 22.6 %copy-start.2 = (bf16[8,2,16,1024]{3,2,1,0:T(8,128)(2,1)}, bf16[8,2,16,1024]{3,2,1,0:T(8,128)(2,1)S(1)}, u32[]{:S(2)}) copy-start(bf16[8,2,16,1024]{3,2,1,0:T(8,128)(2,1)S(1)} %all-to-all-done.2.queries) | copy-start | bytes 1572868
  88.0 82.5 %all-to-all-start.1 = ((bf16[8,2,144,128]{3,2,1,0:T(8,128)(2,1)}), bf16[8,2,144,128]{3,2,1,0:T(8,128)(2,1)S(1)}, u32[]{:S(2)}, u32[]{:S(2)}) async-start(bf16[8,2,144,128]{3,2,1,0:T(8,128)(2,1)} %attend.2), calls=%async_computation.1 | async-start | bytes 1179648 | tf_op jit(solution)/shard_map/all_to_all | solution.py:311
  170.4 38.3 %copy-start = (bf16[8,2,144,128]{3,2,1,0:T(8,128)(2,1)}, bf16[8,2,144,128]{3,2,1,0:T(8,128)(2,1)S(1)}, u32[]{:S(2)}) copy-start(bf16[8,2,144,128]{3,2,1,0:T(8,128)(2,1)S(1)} %all-to-all-done.1.first) | copy-start | bytes 1769476

commit v3 on v2

--- a/solution.py
+++ b/solution.py
@@ -7,12 +7,14 @@
 from jax.experimental.pallas import tpu as pltpu
 from jax.sharding import PartitionSpec as P
 
+
 HEAD = 128
 SCALE = HEAD ** (-0.5) * 1.4426950408889634
 KEYS = 256
 SMALL = 2.0**-60
 LARGE = 2.0**100
 PAD = 16
+TERMS = 4
 
 
 def prepare(me, tile_blocks, block_place, tile_offset, values, turned, slots, *, tile_rows):
@@ -95,22 +97,25 @@
         high = mass.astype(jnp.bfloat16)
         middle = (mass - high.astype(jnp.float32)).astype(jnp.bfloat16)
         low = (mass - high.astype(jnp.float32) - middle.astype(jnp.float32)).astype(jnp.bfloat16)
-        pad = lax.broadcasted_iota(jnp.int32, (PAD, columns), 0)
+        pad = lax.broadcasted_iota(jnp.int32, (TERMS * batches, columns), 0)
         terms = jnp.where(
-            pad == 0,
+            pad % TERMS == 0,
             high.astype(jnp.float32),
             jnp.where(
-                pad == 1,
+                pad % TERMS == 1,
                 middle.astype(jnp.float32),
-                jnp.where(pad == 2, low.astype(jnp.float32), 0.0),
+                jnp.where(pad % TERMS == 2, low.astype(jnp.float32), 0.0),
             ),
-        ).astype(jnp.bfloat16)
+        )
         blended = (total[:HEAD] * (1.0 / summed)).T.astype(jnp.bfloat16)
         for side in range(2):
             device, batch = tile_of(pair, side)
             part = slice(side * rows, (side + 1) * rows)
-            partial[device, batch, :rows] = blended[part]
-            partial[device, batch, rows:] = terms[:, part]
+            partial[device, pl.ds(pl.multiple_of(batch * rows, rows), rows)] = blended[part]
+            held = partial[device, batches * rows :].astype(jnp.float32)
+            partial[device, batches * rows :] = jnp.where(
+                pad[:, part] // TERMS == batch, terms[:, part], held
+            ).astype(jnp.bfloat16)
 
     def quick(first, last, masked, accumulators):
         score = accumulators[:2], accumulators[2:4]
@@ -220,39 +225,47 @@
     )
 
 
-def combine(me, tile_blocks, block_place, first, second, attended):
-    devices, batches, padded, _ = first.shape
+def combine(me, tile_blocks, block_place, returned, *rest, tile_rows):
+    attended = rest[-1]
+    devices, padded, _ = returned.shape
+    batches = attended.shape[0]
     top = tile_blocks.shape[1]
-    rows = padded - PAD
-    tile_rows = attended.shape[1]
+    rows = padded // batches - TERMS
+    start = 0
+    for earlier in rest[:-1]:
+        attended[:, :, : earlier.shape[2]] = earlier[...]
+        start = earlier.shape[2]
     for batch in range(batches):
         owners = [
             block_place[tile_blocks[batch * devices + me[0], entry]] for entry in range(top)
         ]
-        for half, returned in enumerate((first, second)):
-            masses = []
-            for owner in owners:
-                terms = returned[owner, batch, rows:].astype(jnp.float32)
-                masses.append(terms[0:1] + terms[1:2] + terms[2:3])
-            highest = functools.reduce(jnp.maximum, masses)
-            shares = [jnp.exp2(mass - highest) for mass in masses]
-            inverse = 1.0 / functools.reduce(jnp.add, shares)
-            stacked = jnp.concatenate([share * inverse for share in shares], axis=0)
-            stacked = jnp.concatenate(
-                [stacked, jnp.zeros((8 - top, rows), jnp.float32)], axis=0
-            ).T
-            blended = functools.reduce(
-                jnp.add,
-                [
-                    stacked[:, entry : entry + 1] * returned[owner, batch, :rows].astype(jnp.float32)
-                    for entry, owner in enumerate(owners)
-                ],
-            ).astype(jnp.bfloat16)
-            for part in range(rows // tile_rows):
-                column = (half * (rows // tile_rows) + part) * HEAD
-                attended[batch, :, column : column + HEAD] = blended[
-                    part * tile_rows : (part + 1) * tile_rows
-                ]
+        masses = []
+        for owner in owners:
+            terms = returned[owner, batches * rows :].astype(jnp.float32)
+            first = batch * TERMS
+            masses.append(
+                terms[first : first + 1] + terms[first + 1 : first + 2] + terms[first + 2 : first + 3]
+            )
+        highest = functools.reduce(jnp.maximum, masses)
+        shares = [jnp.exp2(mass - highest) for mass in masses]
+        inverse = 1.0 / functools.reduce(jnp.add, shares)
+        stacked = jnp.concatenate(
+            [share * inverse for share in shares] + [jnp.zeros((8 - top, rows), jnp.float32)],
+            axis=0,
+        ).T
+        blended = functools.reduce(
+            jnp.add,
+            [
+                stacked[:, entry : entry + 1]
+                * returned[owner, batch * rows : (batch + 1) * rows].astype(jnp.float32)
+                for entry, owner in enumerate(owners)
+            ],
+        ).astype(jnp.bfloat16)
+        for part in range(rows // tile_rows):
+            column = start + part * HEAD
+            attended[batch, :, column : column + HEAD] = blended[
+                part * tile_rows : (part + 1) * tile_rows
+            ]
 
 
 def local(queries, keys, values, tile_blocks, block_place, tile_offset):
@@ -290,7 +303,7 @@
             functools.partial(attend, tiles=tiles),
             grid=(1,),
             out_shape=jax.ShapeDtypeStruct(
-                (devices, batches, rows + PAD, HEAD), jnp.bfloat16
+                (devices, batches * (rows + TERMS), HEAD), jnp.bfloat16
             ),
             in_specs=[
                 smem,
@@ -310,14 +323,23 @@
         returned.append(
             lax.all_to_all(partial, "seq", split_axis=0, concat_axis=0, tiled=True)
         )
-    out = pl.pallas_call(
-        combine,
-        out_shape=jax.ShapeDtypeStruct((batches, tile_rows, features), jnp.bfloat16),
-        in_specs=[smem, smem, smem, vmem, vmem],
-        out_specs=vmem,
-        name="combine",
-    )(me, tile_blocks, block_place, *returned)
-    return out[:, None]
+    out = ()
+    for head in range(shared):
+        out = (
+            pl.pallas_call(
+                functools.partial(combine, tile_rows=tile_rows),
+                out_shape=jax.ShapeDtypeStruct(
+                    (batches, tile_rows, (head + 1) * width), jnp.bfloat16
+                ),
+                in_specs=[smem, smem, smem, vmem] + [vmem] * len(out),
+                out_specs=vmem,
+                cost_estimate=pl.CostEstimate(
+                    flops=2 * 10**9, transcendentals=0, bytes_accessed=2**20
+                ),
+                name="combine",
+            )(me, tile_blocks, block_place, returned[head], *out),
+        )
+    return out[0][:, None]
 
 
 def solution(mesh):
@@ -329,6 +351,7 @@
         P("groups"),
         P("groups"),
     )
+
     return jax.shard_map(
         local,
         mesh=mesh,

time: 212 us -> 212 us (level)
  starting transfers between devices: 33.6 us -> 134 us
  Pallas kernels: 126 us -> 52.1 us
  blocking collectives: 38.3 us -> 0 us
  waiting for transfers between devices: 8.9 us -> 20.7 us
    all_to_all x1 -> x2, starting transfers between devices: 22.6 us -> 123 us  [local(): lax.all_to_all(partial, 'seq', split_axis=0, concat_axis=0, tiled=True)]
    pallas_call x2, Pallas kernels: 120 us -> 43.8 us  [local(): pl.pallas_call(functools.partial(attend, tiles=tiles), grid=(1,), out_sha...]
    all_to_all x1 -> x0, blocking collectives: 38.3 us -> none  [local(): lax.all_to_all(partial, 'seq', split_axis=0, concat_axis=0, tiled=True)]
    all_to_all x1 -> x2, waiting for transfers between devices: 0.01 us -> 11.9 us  [local(): lax.all_to_all(partial, 'seq', split_axis=0, concat_axis=0, tiled=True)]
  transfers between devices with their start and end apart: 3 -> 4, of which waited for: 1 -> 2; matrix products, arithmetic and copies ran while one was open for 1% -> 1% of each run, Pallas kernels for 59% -> 24%
where the time goes in v3:
time: 212 us
  starting transfers between devices  134 us (63%)
  Pallas kernels  52.1 us (25%)
  waiting for transfers between devices  20.7 us (10%)
  local copies, waits for them, and re-layouts  4.84 us (2%)
    all_to_all x2, starting transfers between devices, local(): lax.all_to_all(partial, 'seq', split_axis=0, concat_axis=0, tiled=True)  123 us
    pallas_call x2, Pallas kernels, local(): pl.pallas_call(functools.partial(attend, tiles=tiles), grid=(1,), out_sha...  43.8 us
    all_to_all x2, waiting for transfers between devices, local(): lax.all_to_all(partial, 'seq', split_axis=0, concat_axis=0, tiled=True)  11.9 us
    all_to_all x2, starting transfers between devices, local(): lax.all_to_all(outgoing, 'seq', split_axis=0, concat_axis=0, tiled=True)  10.9 us
    all_to_all x2, waiting for transfers between devices, local(): lax.all_to_all(outgoing, 'seq', split_axis=0, concat_axis=0, tiled=True)  8.88 us
    pallas_call x1, Pallas kernels, local(): pl.pallas_call(functools.partial(prepare, tile_rows=tile_rows), out_shape...  4.25 us
  transfers between devices with their start and end apart: 4, of which 2 were waited for; matrix products, arithmetic and copies ran while one was open for 1% of the time, Pallas kernels for 24%

profile of v3, /device:TPU:0, one launch (start us, length us, event | category | flops | bytes accessed | tf_op | source)
XLA Modules:
  0.0 211.8 jit_solution(442821080084199570)
XLA Ops:
  0.0 0.9 slice_bitcast_fusion
  0.9 0.9 broadcast_in_dim.24
  1.8 7.3 %all-to-all-start.2 = ((bf16[8,2,16,1024]{3,2,1,0:T(8,128)(2,1)}), bf16[8,2,16,1024]{3,2,1,0:T(8,128)(2,1)S(1)}, u32[]{:S(2)}, u32[]{:S(2)}) async-start(bf16[8,2,16,1024]{3,2,1,0:T(8,128)(2,1)} %broadcast_in_dim.24), calls=%async_computation.2 | async-start | bytes 1048576 | tf_op jit(solution)/shard_map/all_to_all | solution.py:298
  9.0 1.4 copy.9.tile_blocks
  10.4 4.2 %prepare.1 = (bf16[2,144,4096]{2,1,0:T(8,128)(2,1)}, s32[37]{0:T(128)}) custom-call(s32[1]{0:T(128)} %bitcast.me, s32[16,4]{1,0:T(8,128)} %copy.9.tile_blocks, s32[8]{0:T(128)} %block_place.5, s32[16]{0:T(128)} %tile_offset.1, bf16[4096,256]{1,0:T(8,128)(2,1)} %bitcast.9), custom_call_target="tpu_custom_call" | custom-call | flops 10000000000 | bytes 4194304 | tf_op jit(solution)/shard_map/prepare/pallas_call | solution.py:282
  14.6 8.9 %all-to-all-done.2.queries = bf16[8,2,16,1024]{3,2,1,0:T(8,128)(2,1)S(1)} async-done(((bf16[8,2,16,1024]{3,2,1,0:T(8,128)(2,1)}), bf16[8,2,16,1024]{3,2,1,0:T(8,128)(2,1)S(1)}, u32[]{:S(2)}, u32[]{:S(2)}) %all-to-all-start.2) | async-done | bytes 524320 | tf_op jit(solution)/shard_map/all_to_all | solution.py:298
  23.5 0.0 copy-start.2
  23.5 0.9 broadcast_in_dim.22
  24.5 3.6 %all-to-all-start = ((bf16[8,2,16,1024]{3,2,1,0:T(8,128)(2,1)}), bf16[8,2,16,1024]{3,2,1,0:T(8,128)(2,1)S(1)}, u32[]{:S(2)}, u32[]{:S(2)}) async-start(bf16[8,2,16,1024]{3,2,1,0:T(8,128)(2,1)} %broadcast_in_dim.22), calls=%async_computation | async-start | bytes 1048576 | tf_op jit(solution)/shard_map/all_to_all | solution.py:298
  28.1 0.0 copy-done.2
  28.1 21.9 %attend.3 = bf16[8,264,128]{2,1,0:T(8,128)(2,1)} custom-call(s32[37]{0:T(128)} %get-tuple-element.7.slots, bf16[8,2,16,1024]{3,2,1,0:T(8,128)(2,1)} %copy-done.2, bf16[1,4096,256]{2,1,0:T(8,128)(2,1)} %keys_ref.3, bf16[2,144,4096]{2,1,0:T(8,128)(2,1)} %get-tuple-element.8.turned), custom_call_target="tpu_custom_call" | custom-call | flops 10000000000 | bytes 4194304 | tf_op jit(solution)/shard_map/attend/pallas_call | solution.py:302
  50.0 0.0 all-to-all-done.queries
  50.0 0.0 copy-start.3
  50.0 61.6 %all-to-all-start.3 = ((bf16[8,264,128]{2,1,0:T(8,128)(2,1)}), bf16[8,264,128]{2,1,0:T(8,128)(2,1)S(1)}, u32[]{:S(2)}, u32[]{:S(2)}) async-start(bf16[8,264,128]{2,1,0:T(8,128)(2,1)} %attend.3), calls=%async_computation.3 | async-start | bytes 1081344 | tf_op jit(solution)/shard_map/all_to_all | solution.py:324
  111.6 0.0 copy-done.3
  111.6 21.9 %attend.2 = bf16[8,264,128]{2,1,0:T(8,128)(2,1)} custom-call(s32[37]{0:T(128)} %get-tuple-element.7.slots, bf16[8,2,16,1024]{3,2,1,0:T(8,128)(2,1)} %copy-done.3, bf16[1,4096,256]{2,1,0:T(8,128)(2,1)} %keys_ref.3, bf16[2,144,4096]{2,1,0:T(8,128)(2,1)} %get-tuple-element.8.turned), custom_call_target="tpu_custom_call" | custom-call | flops 10000000000 | bytes 4194304 | tf_op jit(solution)/shard_map/attend/pallas_call | solution.py:302
  133.5 0.0 all-to-all-done.3.returned
  133.5 0.0 copy-start
  133.5 61.6 %all-to-all-start.1 = ((bf16[8,264,128]{2,1,0:T(8,128)(2,1)}), bf16[8,264,128]{2,1,0:T(8,128)(2,1)S(1)}, u32[]{:S(2)}, u32[]{:S(2)}) async-start(bf16[8,264,128]{2,1,0:T(8,128)(2,1)} %attend.2), calls=%async_computation.1 | async-start | bytes 1081344 | tf_op jit(solution)/shard_map/all_to_all | solution.py:324
  195.1 0.0 copy-done
  195.1 2.0 combine.2.rest_0_
  197.1 11.9 %all-to-all-done.1.returned = bf16[8,264,128]{2,1,0:T(8,128)(2,1)S(1)} async-done(((bf16[8,264,128]{2,1,0:T(8,128)(2,1)}), bf16[8,264,128]{2,1,0:T(8,128)(2,1)S(1)}, u32[]{:S(2)}, u32[]{:S(2)}) %all-to-all-start.1) | async-done | bytes 540704 | tf_op jit(solution)/shard_map/all_to_all | solution.py:324
  209.0 0.0 copy-start.1
  209.0 0.8 copy-done.1
  209.7 2.1 combine.3
Async XLA Ops:
  1.8 21.8 %all-to-all-start.2 = ((bf16[8,2,16,1024]{3,2,1,0:T(8,128)(2,1)}), bf16[8,2,16,1024]{3,2,1,0:T(8,128)(2,1)S(1)}, u32[]{:S(2)}, u32[]{:S(2)}) async-start(bf16[8,2,16,1024]{3,2,1,0:T(8,128)(2,1)} %broadcast_in_dim.24), calls=%async_computation.2 | async-start | bytes 1048576 | tf_op jit(solution)/shard_map/all_to_all | solution.py:298
  23.5 4.6 %copy-start.2 = (bf16[8,2,16,1024]{3,2,1,0:T(8,128)(2,1)}, bf16[8,2,16,1024]{3,2,1,0:T(8,128)(2,1)S(1)}, u32[]{:S(2)}) copy-start(bf16[8,2,16,1024]{3,2,1,0:T(8,128)(2,1)S(1)} %all-to-all-done.2.queries) | copy-start | bytes 1572868
  24.5 25.5 %all-to-all-start = ((bf16[8,2,16,1024]{3,2,1,0:T(8,128)(2,1)}), bf16[8,2,16,1024]{3,2,1,0:T(8,128)(2,1)S(1)}, u32[]{:S(2)}, u32[]{:S(2)}) async-start(bf16[8,2,16,1024]{3,2,1,0:T(8,128)(2,1)} %broadcast_in_dim.22), calls=%async_computation | async-start | bytes 1048576 | tf_op jit(solution)/shard_map/all_to_all | solution.py:298
  50.0 61.6 %copy-start.3 = (bf16[8,2,16,1024]{3,2,1,0:T(8,128)(2,1)}, bf16[8,2,16,1024]{3,2,1,0:T(8,128)(2,1)S(1)}, u32[]{:S(2)}) copy-start(bf16[8,2,16,1024]{3,2,1,0:T(8,128)(2,1)S(1)} %all-to-all-done.queries) | copy-start | bytes 1572868
  50.0 83.5 %all-to-all-start.3 = ((bf16[8,264,128]{2,1,0:T(8,128)(2,1)}), bf16[8,264,128]{2,1,0:T(8,128)(2,1)S(1)}, u32[]{:S(2)}, u32[]{:S(2)}) async-start(bf16[8,264,128]{2,1,0:T(8,128)(2,1)} %attend.3), calls=%async_computation.3 | async-start | bytes 1081344 | tf_op jit(solution)/shard_map/all_to_all | solution.py:324
  133.5 61.6 %copy-start = (bf16[8,264,128]{2,1,0:T(8,128)(2,1)}, bf16[8,264,128]{2,1,0:T(8,128)(2,1)S(1)}, u32[]{:S(2)}) copy-start(bf16[8,264,128]{2,1,0:T(8,128)(2,1)S(1)} %all-to-all-done.3.returned) | copy-start | bytes 1622020
  133.5 75.5 %all-to-all-start.1 = ((bf16[8,264,128]{2,1,0:T(8,128)(2,1)}), bf16[8,264,128]{2,1,0:T(8,128)(2,1)S(1)}, u32[]{:S(2)}, u32[]{:S(2)}) async-start(bf16[8,264,128]{2,1,0:T(8,128)(2,1)} %attend.2), calls=%async_computation.1 | async-start | bytes 1081344 | tf_op jit(solution)/shard_map/all_to_all | solution.py:324
  209.0 0.8 copy-start.1

commit v4 on v3

--- a/solution.py
+++ b/solution.py
@@ -11,9 +11,9 @@
 HEAD = 128
 SCALE = HEAD ** (-0.5) * 1.4426950408889634
 KEYS = 256
+GRANT = 36 * 2**20
 SMALL = 2.0**-60
 LARGE = 2.0**100
-PAD = 16
 TERMS = 4
 
 
@@ -21,12 +21,9 @@
     keys, features = values.shape
     for head in range(features // HEAD):
         for start in range(0, keys, 512):
-            turned[head, :HEAD, start : start + 512] = values[
+            turned[head, :, start : start + 512] = values[
                 start : start + 512, head * HEAD : (head + 1) * HEAD
             ].T
-        turned[head, HEAD:, :] = jnp.where(
-            lax.broadcasted_iota(jnp.int32, (PAD, keys), 0) == 0, 1.0, 0.0
-        ).astype(turned.dtype)
     block_count = block_place.shape[0]
     tiles, top = tile_blocks.shape
 
@@ -60,11 +57,13 @@
         slots[3 + tiles + count] = slots[2 + tiles + count]
 
 
-def attend(slots, queries, keys_ref, turned, partial, rotated, total, checks, *, tiles):
+def attend(slots, queries, all_keys, turned, partial, rotated, total, checks, *, tiles, head):
     devices, batches, tile_rows, width = queries.shape
     group = width // HEAD
     rows = tile_rows * group
-    key_count = keys_ref.shape[0]
+    keys_ref = all_keys.at[:, head * HEAD : (head + 1) * HEAD]
+    turned = turned.at[head]
+    key_count = all_keys.shape[0]
     columns = 2 * rows
     steps = key_count // (2 * KEYS)
     checks[...] = jnp.ones(checks.shape, jnp.float32)
@@ -136,10 +135,11 @@
                 weights = jnp.where(visible(start, limits), weights, 0.0)
             pltpu.matmul_push_rhs(weights.astype(jnp.bfloat16), 1, unit)
             pltpu.matmul_acc_lhs(value[unit], turned[:, start : start + KEYS], 1)
+            return jnp.sum(weights.reshape(KEYS // 8, 8, columns), axis=0)
 
         def close(pair, real):
-            total[...] = pltpu.matmul_pop(value[0]) + pltpu.matmul_pop(value[1])
-            summed = total[HEAD : HEAD + 1, :]
+            total[:HEAD] = pltpu.matmul_pop(value[0]) + pltpu.matmul_pop(value[1])
+            summed = jnp.sum(total[HEAD:], axis=0, keepdims=True)
             good = (summed > SMALL) & (summed < LARGE)
             checks[...] = jnp.minimum(checks[...], jnp.where(good | jnp.logical_not(real), 1.0, 0.0))
             finish(pair, summed, 0.0)
@@ -147,6 +147,7 @@
         for unit in range(2):
             for accumulator in score[unit] + value[unit : unit + 1]:
                 pltpu.matmul_pop(accumulator)
+        total[HEAD:] = jnp.ones((8, columns), jnp.float32)
         load(first, first % 2)
         for unit in range(2):
             score_step(unit, first % 2, 0)
@@ -162,7 +163,9 @@
                         score_step(unit, place, step + 1)
                     else:
                         score_step(unit, 1 - place, 0)
-                    value_step(unit, step, limits)
+                    added = value_step(unit, step, limits)
+                    whole = added if step + unit == 0 else whole + added
+            total[HEAD:] = whole
             return carry
 
         lax.fori_loop(first, last, body, 0)
@@ -190,17 +193,19 @@
             0, key_count // KEYS, highest_of, jnp.full((1, columns), -1e30, jnp.float32)
         )
 
-        def add(step, carry):
-            weights = jnp.exp2(measured(step) - highest).astype(jnp.bfloat16)
-            pltpu.matmul_push_rhs(weights, 1, 0)
+        def add(step, summed):
+            weights = jnp.exp2(measured(step) - highest)
+            pltpu.matmul_push_rhs(weights.astype(jnp.bfloat16), 1, 0)
             pltpu.matmul_acc_lhs(
                 value, turned[:, pl.ds(pl.multiple_of(step * KEYS, KEYS), KEYS)], 1
             )
-            return carry
-
-        lax.fori_loop(0, key_count // KEYS, add, 0)
-        total[...] = pltpu.matmul_pop(value)
-        finish(pair, total[HEAD : HEAD + 1, :], highest)
+            return summed + jnp.sum(weights, axis=0, keepdims=True)
+
+        summed = lax.fori_loop(
+            0, key_count // KEYS, add, jnp.zeros((1, columns), jnp.float32)
+        )
+        total[:HEAD] = pltpu.matmul_pop(value)
+        finish(pair, summed, highest)
         return carry
 
     def every(*accumulators):
@@ -221,18 +226,18 @@
     pl.run_scoped(
         every,
         *[pltpu.ACC(unit)((KEYS, columns), jnp.float32) for unit in (0, 0, 1, 1)],
-        *[pltpu.ACC(unit)((HEAD + PAD, columns), jnp.float32) for unit in (0, 1)],
+        *[pltpu.ACC(unit)((HEAD, columns), jnp.float32) for unit in (0, 1)],
     )
 
 
 def combine(me, tile_blocks, block_place, returned, *rest, tile_rows):
-    attended = rest[-1]
+    *rest, attended = rest
     devices, padded, _ = returned.shape
     batches = attended.shape[0]
     top = tile_blocks.shape[1]
     rows = padded // batches - TERMS
     start = 0
-    for earlier in rest[:-1]:
+    for earlier in rest:
         attended[:, :, : earlier.shape[2]] = earlier[...]
         start = earlier.shape[2]
     for batch in range(batches):
@@ -268,6 +273,10 @@
             ]
 
 
+def near(array):
+    return pltpu.with_memory_space_constraint(array, pltpu.VMEM)
+
+
 def local(queries, keys, values, tile_blocks, block_place, tile_offset):
     devices = lax.axis_size("seq")
     batches, _, tile_rows, features = queries.shape
@@ -282,44 +291,48 @@
     turned, slots = pl.pallas_call(
         functools.partial(prepare, tile_rows=tile_rows),
         out_shape=(
-            jax.ShapeDtypeStruct((shared, HEAD + PAD, key_count), jnp.bfloat16),
+            jax.ShapeDtypeStruct((shared, HEAD, key_count), jnp.bfloat16),
             jax.ShapeDtypeStruct((2 * tiles + 5,), jnp.int32),
         ),
         in_specs=[smem, smem, smem, smem, vmem],
         out_specs=(vmem, smem),
         cost_estimate=pl.CostEstimate(flops=10**10, transcendentals=0, bytes_accessed=2**22),
-        name="prepare",
+        compiler_params=pltpu.CompilerParams(vmem_limit_bytes=GRANT),
+            name="prepare",
     )(me, tile_blocks, block_place, tile_offset, values[0])
     arrived = []
     for head in range(shared):
-        tile = queries[:, 0, :, head * width : (head + 1) * width]
+        source = lax.optimization_barrier(queries) if head else queries
+        tile = source[:, 0, :, head * width : (head + 1) * width]
         outgoing = jnp.broadcast_to(tile[None], (devices,) + tile.shape)
         arrived.append(
             lax.all_to_all(outgoing, "seq", split_axis=0, concat_axis=0, tiled=True)
         )
+    close_keys = near(keys[0])
+    close_turned = near(turned)
     returned = []
     for head in range(shared):
         partial = pl.pallas_call(
-            functools.partial(attend, tiles=tiles),
-            grid=(1,),
+            functools.partial(attend, tiles=tiles, head=head),
             out_shape=jax.ShapeDtypeStruct(
                 (devices, batches * (rows + TERMS), HEAD), jnp.bfloat16
             ),
             in_specs=[
                 smem,
                 vmem,
-                pl.BlockSpec((None, key_count, HEAD), lambda i, head=head: (0, 0, head)),
-                pl.BlockSpec((None, HEAD + PAD, key_count), lambda i, head=head: (head, 0, 0)),
+                vmem,
+                vmem,
             ],
             out_specs=vmem,
             scratch_shapes=[
                 pltpu.VMEM((2, 2 * HEAD, 2 * rows), jnp.bfloat16),
-                pltpu.VMEM((HEAD + PAD, 2 * rows), jnp.float32),
+                pltpu.VMEM((HEAD + 8, 2 * rows), jnp.float32),
                 pltpu.VMEM((1, 2 * rows), jnp.float32),
             ],
             cost_estimate=pl.CostEstimate(flops=10**10, transcendentals=0, bytes_accessed=2**22),
+            compiler_params=pltpu.CompilerParams(vmem_limit_bytes=GRANT),
             name="attend",
-        )(slots, arrived[head], keys, turned)
+        )(slots, near(arrived[head]), close_keys, close_turned)
         returned.append(
             lax.all_to_all(partial, "seq", split_axis=0, concat_axis=0, tiled=True)
         )
@@ -336,8 +349,9 @@
                 cost_estimate=pl.CostEstimate(
                     flops=2 * 10**9, transcendentals=0, bytes_accessed=2**20
                 ),
-                name="combine",
-            )(me, tile_blocks, block_place, returned[head], *out),
+                compiler_params=pltpu.CompilerParams(vmem_limit_bytes=GRANT),
+            name="combine",
+            )(me, tile_blocks, block_place, near(returned[head]), *out),
         )
     return out[0][:, None]
 

time: 212 us -> 210 us (level)
  local copies, waits for them, and re-layouts: 4.84 us -> 11.6 us
  Pallas kernels: 52.1 us -> 47.1 us
    unnamed x9 -> x17, local copies, waits for them, and re-layouts: 2.16 us -> 8.16 us
    all_to_all x2, waiting for transfers between devices: 8.88 us -> 6.14 us  [local(): lax.all_to_all(outgoing, 'seq', split_axis=0, concat_axis=0, tiled=True)]
    all_to_all x2, starting transfers between devices: 123 us -> 121 us  [local(): lax.all_to_all(partial, 'seq', split_axis=0, concat_axis=0, tiled=True)]
  transfers between devices with their start and end apart: 4 -> 4, of which waited for: 2 -> 2; matrix products, arithmetic and copies ran while one was open for 1% -> 1% of each run, Pallas kernels for 24% -> 22%
where the time goes in v4:
time: 210 us; the launch traced here: 209 us
  starting transfers between devices  132 us (63%)
  Pallas kernels  47.1 us (22%)
  waiting for transfers between devices  19 us (9%)
  local copies, waits for them, and re-layouts  11.6 us (6%)
    all_to_all x2, starting transfers between devices, local(): lax.all_to_all(partial, 'seq', split_axis=0, concat_axis=0, tiled=True)  121 us
    pallas_call x2, Pallas kernels, local(): pl.pallas_call(functools.partial(attend, tiles=tiles, head=head), out_sha...  41.9 us
    all_to_all x2, waiting for transfers between devices, local(): lax.all_to_all(partial, 'seq', split_axis=0, concat_axis=0, tiled=True)  12.9 us
    all_to_all x2, starting transfers between devices, local(): lax.all_to_all(outgoing, 'seq', split_axis=0, concat_axis=0, tiled=True)  10.9 us
    unnamed x17, local copies, waits for them, and re-layouts  8.16 us
    all_to_all x2, waiting for transfers between devices, local(): lax.all_to_all(outgoing, 'seq', split_axis=0, concat_axis=0, tiled=True)  6.14 us
  transfers between devices with their start and end apart: 4, of which 2 were waited for; matrix products, arithmetic and copies ran while one was open for 1% of the time, Pallas kernels for 22%

profile of v4, /device:TPU:0, one launch (start us, length us, event | category | flops | bytes accessed | tf_op | source)
XLA Modules:
  0.0 209.5 jit_solution(6651770729586365002)
XLA Ops:
  0.0 0.8 slice_bitcast_fusion.1
  0.8 0.9 broadcast_in_dim.24
  1.7 7.3 %all-to-all-start.2 = ((bf16[8,2,16,1024]{3,2,1,0:T(8,128)(2,1)}), bf16[8,2,16,1024]{3,2,1,0:T(8,128)(2,1)S(1)}, u32[]{:S(2)}, u32[]{:S(2)}) async-start(bf16[8,2,16,1024]{3,2,1,0:T(8,128)(2,1)} %broadcast_in_dim.24), calls=%async_computation.2 | async-start | bytes 1048576 | tf_op jit(solution)/shard_map/all_to_all | solution.py:309
  9.0 0.8 copy.9.tile_blocks
  9.8 0.8 slice_bitcast_fusion
  10.6 0.0 copy-start
  10.6 1.6 copy-done
  12.2 0.0 copy-start.2
  12.2 0.7 copy-done.2
  12.9 0.0 copy-start.3
  12.9 0.7 copy-done.3
  13.5 0.0 copy-start.1
  13.5 2.5 %prepare.1 = (bf16[2,128,4096]{2,1,0:T(8,128)(2,1)S(1)}, s32[37]{0:T(128)S(1)}) custom-call(s32[1]{0:T(128)} %bitcast.me, s32[16,4]{1,0:T(8,128)S(1)} %copy.9.tile_blocks, s32[8]{0:T(128)S(1)} %copy-done.3, s32[16]{0:T(128)S(1)} %copy-done.2, bf16[4096,256]{1,0:T(8,128)(2,1)S(1)} %bitcast.10), custom_call_target="tpu_custom_call" | custom-call | flops 10000000000 | bytes 4194304 | tf_op jit(solution)/shard_map/prepare/pallas_call | solution.py:291
  16.0 0.0 copy-start.5
  16.0 1.3 copy-done.5
  17.4 6.1 %all-to-all-done.2.queries = bf16[8,2,16,1024]{3,2,1,0:T(8,128)(2,1)S(1)} async-done(((bf16[8,2,16,1024]{3,2,1,0:T(8,128)(2,1)}), bf16[8,2,16,1024]{3,2,1,0:T(8,128)(2,1)S(1)}, u32[]{:S(2)}, u32[]{:S(2)}) %all-to-all-start.2) | async-done | bytes 524320 | tf_op jit(solution)/shard_map/all_to_all | solution.py:309
  23.5 0.9 broadcast_in_dim.22
  24.4 3.6 %all-to-all-start = ((bf16[8,2,16,1024]{3,2,1,0:T(8,128)(2,1)}), bf16[8,2,16,1024]{3,2,1,0:T(8,128)(2,1)S(1)}, u32[]{:S(2)}, u32[]{:S(2)}) async-start(bf16[8,2,16,1024]{3,2,1,0:T(8,128)(2,1)} %broadcast_in_dim.22), calls=%async_computation | async-start | bytes 1048576 | tf_op jit(solution)/shard_map/all_to_all | solution.py:309
  28.0 0.0 copy-done.1
  28.0 0.0 copy-start.6
  28.0 1.6 copy-done.6
  29.6 21.0 %attend.3 = bf16[8,264,128]{2,1,0:T(8,128)(2,1)} custom-call(s32[37]{0:T(128)S(1)} %get-tuple-element.7.slots, bf16[8,2,16,1024]{3,2,1,0:T(8,128)(2,1)S(1)} %all-to-all-done.2.queries, bf16[4096,256]{1,0:T(8,128)(2,1)S(1)} %bitcast.11, bf16[2,128,4096]{2,1,0:T(8,128)(2,1)S(1)} %copy-done.6), custom_call_target="tpu_custom_call" | custom-call | flops 10000000000 | bytes 4194304 | tf_op jit(solution)/shard_map/attend/pallas_call | solution.py:315
  50.6 0.0 all-to-all-done.queries
  50.6 60.4 %all-to-all-start.3 = ((bf16[8,264,128]{2,1,0:T(8,128)(2,1)}), bf16[8,264,128]{2,1,0:T(8,128)(2,1)S(1)}, u32[]{:S(2)}, u32[]{:S(2)}) async-start(bf16[8,264,128]{2,1,0:T(8,128)(2,1)} %attend.3), calls=%async_computation.3 | async-start | bytes 1081344 | tf_op jit(solution)/shard_map/all_to_all | solution.py:337
  110.9 0.0 copy-start.7
  111.0 1.6 copy-done.7
  112.5 0.0 copy-start.4
  112.5 20.9 %attend.2 = bf16[8,264,128]{2,1,0:T(8,128)(2,1)} custom-call(s32[37]{0:T(128)S(1)} %get-tuple-element.7.slots, bf16[8,2,16,1024]{3,2,1,0:T(8,128)(2,1)S(1)} %all-to-all-done.queries, bf16[4096,256]{1,0:T(8,128)(2,1)S(1)} %bitcast.12, bf16[2,128,4096]{2,1,0:T(8,128)(2,1)S(1)} %copy-done.7), custom_call_target="tpu_custom_call" | custom-call | flops 10000000000 | bytes 4194304 | tf_op jit(solution)/shard_map/attend/pallas_call | solution.py:315
  133.5 0.0 all-to-all-done.3.returned
  133.5 60.5 %all-to-all-start.1 = ((bf16[8,264,128]{2,1,0:T(8,128)(2,1)}), bf16[8,264,128]{2,1,0:T(8,128)(2,1)S(1)}, u32[]{:S(2)}, u32[]{:S(2)}) async-start(bf16[8,264,128]{2,1,0:T(8,128)(2,1)} %attend.2), calls=%async_computation.1 | async-start | bytes 1081344 | tf_op jit(solution)/shard_map/all_to_all | solution.py:337
  194.0 0.0 copy-done.4
  194.0 1.0 combine.2.rest_0_
  195.0 12.9 %all-to-all-done.1.returned = bf16[8,264,128]{2,1,0:T(8,128)(2,1)S(1)} async-done(((bf16[8,264,128]{2,1,0:T(8,128)(2,1)}), bf16[8,264,128]{2,1,0:T(8,128)(2,1)S(1)}, u32[]{:S(2)}, u32[]{:S(2)}) %all-to-all-start.1) | async-done | bytes 540704 | tf_op jit(solution)/shard_map/all_to_all | solution.py:337
  207.8 1.7 combine.3
Async XLA Ops:
  1.7 21.8 %all-to-all-start.2 = ((bf16[8,2,16,1024]{3,2,1,0:T(8,128)(2,1)}), bf16[8,2,16,1024]{3,2,1,0:T(8,128)(2,1)S(1)}, u32[]{:S(2)}, u32[]{:S(2)}) async-start(bf16[8,2,16,1024]{3,2,1,0:T(8,128)(2,1)} %broadcast_in_dim.24), calls=%async_computation.2 | async-start | bytes 1048576 | tf_op jit(solution)/shard_map/all_to_all | solution.py:309
  10.6 1.6 copy-start
  12.2 0.7 copy-start.2
  12.9 0.7 copy-start.3
  13.5 14.5 %copy-start.1 = (bf16[1,4096,256]{2,1,0:T(8,128)(2,1)S(1)}, bf16[1,4096,256]{2,1,0:T(8,128)(2,1)}, u32[]{:S(2)}) copy-start(bf16[1,4096,256]{2,1,0:T(8,128)(2,1)} %param.7) | copy-start | bytes 6291460
  16.0 1.3 copy-start.5
  24.4 26.2 %all-to-all-start = ((bf16[8,2,16,1024]{3,2,1,0:T(8,128)(2,1)}), bf16[8,2,16,1024]{3,2,1,0:T(8,128)(2,1)S(1)}, u32[]{:S(2)}, u32[]{:S(2)}) async-start(bf16[8,2,16,1024]{3,2,1,0:T(8,128)(2,1)} %broadcast_in_dim.22), calls=%async_computation | async-start | bytes 1048576 | tf_op jit(solution)/shard_map/all_to_all | solution.py:309
  28.0 1.6 copy-start.6
  50.6 82.9 %all-to-all-start.3 = ((bf16[8,264,128]{2,1,0:T(8,128)(2,1)}), bf16[8,264,128]{2,1,0:T(8,128)(2,1)S(1)}, u32[]{:S(2)}, u32[]{:S(2)}) async-start(bf16[8,264,128]{2,1,0:T(8,128)(2,1)} %attend.3), calls=%async_computation.3 | async-start | bytes 1081344 | tf_op jit(solution)/shard_map/all_to_all | solution.py:337
  110.9 1.6 copy-start.7
  112.5 81.4 %copy-start.4 = (s32[8]{0:T(128)S(1)}, s32[8]{0:T(128)}, u32[]{:S(2)}) copy-start(s32[8]{0:T(128)} %block_place.5) | copy-start | bytes 100
  133.5 74.3 %all-to-all-start.1 = ((bf16[8,264,128]{2,1,0:T(8,128)(2,1)}), bf16[8,264,128]{2,1,0:T(8,128)(2,1)S(1)}, u32[]{:S(2)}, u32[]{:S(2)}) async-start(bf16[8,264,128]{2,1,0:T(8,128)(2,1)} %attend.2), calls=%async_computation.1 | async-start | bytes 1081344 | tf_op jit(solution)/shard_map/all_to_all | solution.py:337

commit v5 on v4

--- a/solution.py
+++ b/solution.py
@@ -57,12 +57,15 @@
         slots[3 + tiles + count] = slots[2 + tiles + count]
 
 
-def attend(slots, queries, all_keys, turned, partial, rotated, total, checks, *, tiles, head):
+def attend(
+    slots, queries, all_keys, both, partial, rotated, total, checks, turned, arrival, *, tiles, head
+):
     devices, batches, tile_rows, width = queries.shape
     group = width // HEAD
     rows = tile_rows * group
     keys_ref = all_keys.at[:, head * HEAD : (head + 1) * HEAD]
-    turned = turned.at[head]
+    copy = pltpu.make_async_copy(both.at[head], turned, arrival)
+    copy.start()
     key_count = all_keys.shape[0]
     columns = 2 * rows
     steps = key_count // (2 * KEYS)
@@ -209,6 +212,8 @@
         return carry
 
     def every(*accumulators):
+        copy.wait()
+
         @pl.when(slots[0] > 0)
         def _():
             quick(0, slots[0], False, accumulators)
@@ -309,7 +314,7 @@
             lax.all_to_all(outgoing, "seq", split_axis=0, concat_axis=0, tiled=True)
         )
     close_keys = near(keys[0])
-    close_turned = near(turned)
+    turned = pltpu.with_memory_space_constraint(turned, pltpu.HBM)
     returned = []
     for head in range(shared):
         partial = pl.pallas_call(
@@ -321,18 +326,20 @@
                 smem,
                 vmem,
                 vmem,
-                vmem,
+                pl.BlockSpec(memory_space=pltpu.HBM),
             ],
             out_specs=vmem,
             scratch_shapes=[
                 pltpu.VMEM((2, 2 * HEAD, 2 * rows), jnp.bfloat16),
                 pltpu.VMEM((HEAD + 8, 2 * rows), jnp.float32),
                 pltpu.VMEM((1, 2 * rows), jnp.float32),
+                pltpu.VMEM((HEAD, key_count), jnp.bfloat16),
+                pltpu.SemaphoreType.DMA,
             ],
             cost_estimate=pl.CostEstimate(flops=10**10, transcendentals=0, bytes_accessed=2**22),
             compiler_params=pltpu.CompilerParams(vmem_limit_bytes=GRANT),
             name="attend",
-        )(slots, near(arrived[head]), close_keys, close_turned)
+        )(slots, near(arrived[head]), close_keys, turned)
         returned.append(
             lax.all_to_all(partial, "seq", split_axis=0, concat_axis=0, tiled=True)
         )

time: 210 us -> 210 us (level)
  local copies, waits for them, and re-layouts: 11.6 us -> 8.42 us
  Pallas kernels: 47.1 us -> 49.5 us
    unnamed x17 -> x13, local copies, waits for them, and re-layouts: 8.16 us -> 5 us
    pallas_call x2, Pallas kernels: 41.9 us -> 44.4 us  [local(): pl.pallas_call(functools.partial(attend, tiles=tiles, head=head), out_sha...]
  transfers between devices with their start and end apart: 4 -> 4, of which waited for: 2 -> 2; matrix products, arithmetic and copies ran while one was open for 1% -> 1% of each run, Pallas kernels for 22% -> 23%
where the time goes in v5:
time: 210 us; the launch traced here: 209 us
  starting transfers between devices  132 us (63%)
  Pallas kernels  49.5 us (24%)
  waiting for transfers between devices  19 us (9%)
  local copies, waits for them, and re-layouts  8.42 us (4%)
    all_to_all x2, starting transfers between devices, local(): lax.all_to_all(partial, 'seq', split_axis=0, concat_axis=0, tiled=True)  121 us
    pallas_call x2, Pallas kernels, local(): pl.pallas_call(functools.partial(attend, tiles=tiles, head=head), out_sha...  44.4 us
    all_to_all x2, waiting for transfers between devices, local(): lax.all_to_all(partial, 'seq', split_axis=0, concat_axis=0, tiled=True)  12.9 us
    all_to_all x2, starting transfers between devices, local(): lax.all_to_all(outgoing, 'seq', split_axis=0, concat_axis=0, tiled=True)  10.9 us
    all_to_all x2, waiting for transfers between devices, local(): lax.all_to_all(outgoing, 'seq', split_axis=0, concat_axis=0, tiled=True)  6.13 us
    unnamed x13, local copies, waits for them, and re-layouts  5 us
  transfers between devices with their start and end apart: 4, of which 2 were waited for; matrix products, arithmetic and copies ran while one was open for 1% of the time, Pallas kernels for 23%

profile of v5, /device:TPU:0, one launch (start us, length us, event | category | flops | bytes accessed | tf_op | source)
XLA Modules:
  0.0 208.8 jit_solution(785118591092980128)
XLA Ops:
  0.0 0.8 slice_bitcast_fusion.1
  0.8 0.9 broadcast_in_dim.24
  1.7 7.3 %all-to-all-start.2 = ((bf16[8,2,16,1024]{3,2,1,0:T(8,128)(2,1)}), bf16[8,2,16,1024]{3,2,1,0:T(8,128)(2,1)S(1)}, u32[]{:S(2)}, u32[]{:S(2)}) async-start(bf16[8,2,16,1024]{3,2,1,0:T(8,128)(2,1)} %broadcast_in_dim.24), calls=%async_computation.2 | async-start | bytes 1048576 | tf_op jit(solution)/shard_map/all_to_all | solution.py:314
  9.0 0.8 copy.9.tile_blocks
  9.7 0.8 slice_bitcast_fusion
  10.6 0.0 copy-start
  10.6 1.6 copy-done
  12.2 0.0 copy-start.2
  12.2 0.7 copy-done.2
  12.8 0.0 copy-start.3
  12.8 0.7 copy-done.3
  13.5 0.0 copy-start.1
  13.5 2.5 %prepare.1 = (bf16[2,128,4096]{2,1,0:T(8,128)(2,1)S(1)}, s32[37]{0:T(128)S(1)}) custom-call(s32[1]{0:T(128)} %bitcast.me, s32[16,4]{1,0:T(8,128)S(1)} %copy.9.tile_blocks, s32[8]{0:T(128)S(1)} %copy-done.3, s32[16]{0:T(128)S(1)} %copy-done.2, bf16[4096,256]{1,0:T(8,128)(2,1)S(1)} %bitcast.10), custom_call_target="tpu_custom_call" | custom-call | flops 10000000000 | bytes 4194304 | tf_op jit(solution)/shard_map/prepare/pallas_call | solution.py:296
  16.0 0.0 copy-start.5
  16.0 1.3 copy-done.5
  17.3 6.1 %all-to-all-done.2.queries = bf16[8,2,16,1024]{3,2,1,0:T(8,128)(2,1)S(1)} async-done(((bf16[8,2,16,1024]{3,2,1,0:T(8,128)(2,1)}), bf16[8,2,16,1024]{3,2,1,0:T(8,128)(2,1)S(1)}, u32[]{:S(2)}, u32[]{:S(2)}) %all-to-all-start.2) | async-done | bytes 524320 | tf_op jit(solution)/shard_map/all_to_all | solution.py:314
  23.5 0.9 broadcast_in_dim.22
  24.3 3.6 %all-to-all-start = ((bf16[8,2,16,1024]{3,2,1,0:T(8,128)(2,1)}), bf16[8,2,16,1024]{3,2,1,0:T(8,128)(2,1)S(1)}, u32[]{:S(2)}, u32[]{:S(2)}) async-start(bf16[8,2,16,1024]{3,2,1,0:T(8,128)(2,1)} %broadcast_in_dim.22), calls=%async_computation | async-start | bytes 1048576 | tf_op jit(solution)/shard_map/all_to_all | solution.py:314
  28.0 0.0 copy-done.1
  28.0 22.2 %attend.3 = bf16[8,264,128]{2,1,0:T(8,128)(2,1)} custom-call(s32[37]{0:T(128)S(1)} %get-tuple-element.7.slots, bf16[8,2,16,1024]{3,2,1,0:T(8,128)(2,1)S(1)} %all-to-all-done.2.queries, bf16[4096,256]{1,0:T(8,128)(2,1)S(1)} %bitcast.11, bf16[2,128,4096]{2,1,0:T(8,128)(2,1)} %copy-done.5), custom_call_target="tpu_custom_call" | custom-call | flops 10000000000 | bytes 4194304 | tf_op jit(solution)/shard_map/attend/pallas_call | solution.py:320
  50.2 0.0 all-to-all-done.queries
  50.2 60.4 %all-to-all-start.3 = ((bf16[8,264,128]{2,1,0:T(8,128)(2,1)}), bf16[8,264,128]{2,1,0:T(8,128)(2,1)S(1)}, u32[]{:S(2)}, u32[]{:S(2)}) async-start(bf16[8,264,128]{2,1,0:T(8,128)(2,1)} %attend.3), calls=%async_computation.3 | async-start | bytes 1081344 | tf_op jit(solution)/shard_map/all_to_all | solution.py:344
  110.6 0.0 copy-start.4
  110.6 22.2 %attend.2 = bf16[8,264,128]{2,1,0:T(8,128)(2,1)} custom-call(s32[37]{0:T(128)S(1)} %get-tuple-element.7.slots, bf16[8,2,16,1024]{3,2,1,0:T(8,128)(2,1)S(1)} %all-to-all-done.queries, bf16[4096,256]{1,0:T(8,128)(2,1)S(1)} %bitcast.12, bf16[2,128,4096]{2,1,0:T(8,128)(2,1)} %copy-done.5), custom_call_target="tpu_custom_call" | custom-call | flops 10000000000 | bytes 4194304 | tf_op jit(solution)/shard_map/attend/pallas_call | solution.py:320
  132.8 0.0 all-to-all-done.3.returned
  132.8 60.5 %all-to-all-start.1 = ((bf16[8,264,128]{2,1,0:T(8,128)(2,1)}), bf16[8,264,128]{2,1,0:T(8,128)(2,1)S(1)}, u32[]{:S(2)}, u32[]{:S(2)}) async-start(bf16[8,264,128]{2,1,0:T(8,128)(2,1)} %attend.2), calls=%async_computation.1 | async-start | bytes 1081344 | tf_op jit(solution)/shard_map/all_to_all | solution.py:344
  193.3 0.0 copy-done.4
  193.3 1.0 combine.2.rest_0_
  194.3 12.9 %all-to-all-done.1.returned = bf16[8,264,128]{2,1,0:T(8,128)(2,1)S(1)} async-done(((bf16[8,264,128]{2,1,0:T(8,128)(2,1)}), bf16[8,264,128]{2,1,0:T(8,128)(2,1)S(1)}, u32[]{:S(2)}, u32[]{:S(2)}) %all-to-all-start.1) | async-done | bytes 540704 | tf_op jit(solution)/shard_map/all_to_all | solution.py:344
  207.2 1.7 combine.3
Async XLA Ops:
  1.7 21.8 %all-to-all-start.2 = ((bf16[8,2,16,1024]{3,2,1,0:T(8,128)(2,1)}), bf16[8,2,16,1024]{3,2,1,0:T(8,128)(2,1)S(1)}, u32[]{:S(2)}, u32[]{:S(2)}) async-start(bf16[8,2,16,1024]{3,2,1,0:T(8,128)(2,1)} %broadcast_in_dim.24), calls=%async_computation.2 | async-start | bytes 1048576 | tf_op jit(solution)/shard_map/all_to_all | solution.py:314
  10.6 1.6 copy-start
  12.2 0.7 copy-start.2
  12.8 0.7 copy-start.3
  13.5 14.5 %copy-start.1 = (bf16[1,4096,256]{2,1,0:T(8,128)(2,1)S(1)}, bf16[1,4096,256]{2,1,0:T(8,128)(2,1)}, u32[]{:S(2)}) copy-start(bf16[1,4096,256]{2,1,0:T(8,128)(2,1)} %param.7) | copy-start | bytes 6291460
  16.0 1.3 copy-start.5
  24.3 25.8 %all-to-all-start = ((bf16[8,2,16,1024]{3,2,1,0:T(8,128)(2,1)}), bf16[8,2,16,1024]{3,2,1,0:T(8,128)(2,1)S(1)}, u32[]{:S(2)}, u32[]{:S(2)}) async-start(bf16[8,2,16,1024]{3,2,1,0:T(8,128)(2,1)} %broadcast_in_dim.22), calls=%async_computation | async-start | bytes 1048576 | tf_op jit(solution)/shard_map/all_to_all | solution.py:314
  50.2 82.6 %all-to-all-start.3 = ((bf16[8,264,128]{2,1,0:T(8,128)(2,1)}), bf16[8,264,128]{2,1,0:T(8,128)(2,1)S(1)}, u32[]{:S(2)}, u32[]{:S(2)}) async-start(bf16[8,264,128]{2,1,0:T(8,128)(2,1)} %attend.3), calls=%async_computation.3 | async-start | bytes 1081344 | tf_op jit(solution)/shard_map/all_to_all | solution.py:344
  110.6 82.7 %copy-start.4 = (s32[8]{0:T(128)S(1)}, s32[8]{0:T(128)}, u32[]{:S(2)}) copy-start(s32[8]{0:T(128)} %block_place.5) | copy-start | bytes 100
  132.8 74.4 %all-to-all-start.1 = ((bf16[8,264,128]{2,1,0:T(8,128)(2,1)}), bf16[8,264,128]{2,1,0:T(8,128)(2,1)S(1)}, u32[]{:S(2)}, u32[]{:S(2)}) async-start(bf16[8,264,128]{2,1,0:T(8,128)(2,1)} %attend.2), calls=%async_computation.1 | async-start | bytes 1081344 | tf_op jit(solution)/shard_map/all_to_all | solution.py:344

commit v6 on v5

--- a/solution.py
+++ b/solution.py
@@ -32,22 +32,24 @@
 
     mine = lax.fori_loop(0, block_count, find, 0)
 
-    def visit(tile, counts, late):
-        count = counts
+    def visit(tile, count, kind):
         entries = [tile_blocks[tile, entry] for entry in range(top)]
         own = functools.reduce(jnp.maximum, entries) == mine
         named = functools.reduce(jnp.logical_or, [entry == mine for entry in entries])
-        chosen = named & (own if late else jnp.logical_not(own))
+        near = tile_offset[tile] * tile_rows + tile_rows <= keys // 2
+        wanted = (jnp.logical_not(own), own & jnp.logical_not(near), own & near)
+        chosen = named & wanted[kind]
 
         @pl.when(chosen)
         def _():
             slots[2 + count] = tile
-            slots[3 + tiles + count] = tile_offset[tile] * tile_rows if late else keys
+            slots[3 + tiles + count] = tile_offset[tile] * tile_rows if kind else keys
 
         return count + chosen.astype(jnp.int32)
 
-    whole = lax.fori_loop(0, tiles, functools.partial(visit, late=False), 0)
-    count = lax.fori_loop(0, tiles, functools.partial(visit, late=True), whole)
+    whole = lax.fori_loop(0, tiles, functools.partial(visit, kind=0), 0)
+    count = lax.fori_loop(0, tiles, functools.partial(visit, kind=1), whole)
+    count = lax.fori_loop(0, tiles, functools.partial(visit, kind=2), count)
     slots[0] = whole // 2
     slots[1] = (count + 1) // 2
 
@@ -160,15 +162,37 @@
             limits = limits_of(pair) if masked else None
             close(jnp.maximum(pair - 1, first), pair > first)
             load(jnp.minimum(pair + 1, last - 1), 1 - place)
-            for step in range(steps):
+
+            def advance(start, stop):
+                added = []
+                for step in range(start, stop):
+                    for unit in range(2):
+                        if step + 1 < steps:
+                            score_step(unit, place, step + 1)
+                        else:
+                            score_step(unit, 1 - place, 0)
+                        added.append(value_step(unit, step, limits))
+                return functools.reduce(jnp.add, added)
+
+            if not masked:
+                total[HEAD:] = advance(0, steps)
+                return carry
+            total[HEAD:] = advance(0, steps // 2)
+            farthest = functools.reduce(
+                jnp.maximum, [slots[3 + tiles + 2 * pair + side] for side in range(2)]
+            )
+            beyond = farthest + tile_rows > key_count // 2
+
+            @pl.when(beyond)
+            def _():
+                total[HEAD:] += advance(steps // 2, steps)
+
+            @pl.when(jnp.logical_not(beyond))
+            def _():
                 for unit in range(2):
-                    if step + 1 < steps:
-                        score_step(unit, place, step + 1)
-                    else:
-                        score_step(unit, 1 - place, 0)
-                    added = value_step(unit, step, limits)
-                    whole = added if step + unit == 0 else whole + added
-            total[HEAD:] = whole
+                    pltpu.matmul_pop(score[unit][steps // 2 % 2])
+                    score_step(unit, 1 - place, 0)
+
             return carry
 
         lax.fori_loop(first, last, body, 0)

time: 210 us -> 210 us (level)
  no operation moved by 1% of the time
where the time goes in v6:
time: 210 us; the launch traced here: 209 us
  starting transfers between devices  132 us (63%)
  Pallas kernels  50 us (24%)
  waiting for transfers between devices  18.7 us (9%)
  local copies, waits for them, and re-layouts  8.42 us (4%)
    all_to_all x2, starting transfers between devices, local(): lax.all_to_all(partial, 'seq', split_axis=0, concat_axis=0, tiled=True)  121 us
    pallas_call x2, Pallas kernels, local(): pl.pallas_call(functools.partial(attend, tiles=tiles, head=head), out_sha...  44.5 us
    all_to_all x2, waiting for transfers between devices, local(): lax.all_to_all(partial, 'seq', split_axis=0, concat_axis=0, tiled=True)  12.9 us
    all_to_all x2, starting transfers between devices, local(): lax.all_to_all(outgoing, 'seq', split_axis=0, concat_axis=0, tiled=True)  10.9 us
    all_to_all x2, waiting for transfers between devices, local(): lax.all_to_all(outgoing, 'seq', split_axis=0, concat_axis=0, tiled=True)  5.8 us
    unnamed x13, local copies, waits for them, and re-layouts  5 us
  transfers between devices with their start and end apart: 4, of which 2 were waited for; matrix products, arithmetic and copies ran while one was open for 1% of the time, Pallas kernels for 23%

profile of v6, /device:TPU:0, one launch (start us, length us, event | category | flops | bytes accessed | tf_op | source)
XLA Modules:
  0.0 208.8 jit_solution(6334766830958447944)
XLA Ops:
  0.0 0.8 slice_bitcast_fusion.1
  0.8 0.9 broadcast_in_dim.24
  1.7 7.3 %all-to-all-start.2 = ((bf16[8,2,16,1024]{3,2,1,0:T(8,128)(2,1)}), bf16[8,2,16,1024]{3,2,1,0:T(8,128)(2,1)S(1)}, u32[]{:S(2)}, u32[]{:S(2)}) async-start(bf16[8,2,16,1024]{3,2,1,0:T(8,128)(2,1)} %broadcast_in_dim.24), calls=%async_computation.2 | async-start | bytes 1048576 | tf_op jit(solution)/shard_map/all_to_all | solution.py:338
  9.0 0.8 copy.9.tile_blocks
  9.7 0.8 slice_bitcast_fusion
  10.6 0.0 copy-start
  10.6 1.6 copy-done
  12.2 0.0 copy-start.2
  12.2 0.7 copy-done.2
  12.8 0.0 copy-start.3
  12.8 0.7 copy-done.3
  13.5 0.0 copy-start.1
  13.5 2.8 %prepare.1 = (bf16[2,128,4096]{2,1,0:T(8,128)(2,1)S(1)}, s32[37]{0:T(128)S(1)}) custom-call(s32[1]{0:T(128)} %bitcast.me, s32[16,4]{1,0:T(8,128)S(1)} %copy.9.tile_blocks, s32[8]{0:T(128)S(1)} %copy-done.3, s32[16]{0:T(128)S(1)} %copy-done.2, bf16[4096,256]{1,0:T(8,128)(2,1)S(1)} %bitcast.10), custom_call_target="tpu_custom_call" | custom-call | flops 10000000000 | bytes 4194304 | tf_op jit(solution)/shard_map/prepare/pallas_call | solution.py:320
  16.3 0.0 copy-start.5
  16.3 1.3 copy-done.5
  17.7 5.8 %all-to-all-done.2.queries = bf16[8,2,16,1024]{3,2,1,0:T(8,128)(2,1)S(1)} async-done(((bf16[8,2,16,1024]{3,2,1,0:T(8,128)(2,1)}), bf16[8,2,16,1024]{3,2,1,0:T(8,128)(2,1)S(1)}, u32[]{:S(2)}, u32[]{:S(2)}) %all-to-all-start.2) | async-done | bytes 524320 | tf_op jit(solution)/shard_map/all_to_all | solution.py:338
  23.5 0.9 broadcast_in_dim.22
  24.3 3.6 %all-to-all-start = ((bf16[8,2,16,1024]{3,2,1,0:T(8,128)(2,1)}), bf16[8,2,16,1024]{3,2,1,0:T(8,128)(2,1)S(1)}, u32[]{:S(2)}, u32[]{:S(2)}) async-start(bf16[8,2,16,1024]{3,2,1,0:T(8,128)(2,1)} %broadcast_in_dim.22), calls=%async_computation | async-start | bytes 1048576 | tf_op jit(solution)/shard_map/all_to_all | solution.py:338
  28.0 0.0 copy-done.1
  28.0 22.3 %attend.3 = bf16[8,264,128]{2,1,0:T(8,128)(2,1)} custom-call(s32[37]{0:T(128)S(1)} %get-tuple-element.7.slots, bf16[8,2,16,1024]{3,2,1,0:T(8,128)(2,1)S(1)} %all-to-all-done.2.queries, bf16[4096,256]{1,0:T(8,128)(2,1)S(1)} %bitcast.11, bf16[2,128,4096]{2,1,0:T(8,128)(2,1)} %copy-done.5), custom_call_target="tpu_custom_call" | custom-call | flops 10000000000 | bytes 4194304 | tf_op jit(solution)/shard_map/attend/pallas_call | solution.py:344
  50.3 0.0 all-to-all-done.queries
  50.3 60.3 %all-to-all-start.3 = ((bf16[8,264,128]{2,1,0:T(8,128)(2,1)}), bf16[8,264,128]{2,1,0:T(8,128)(2,1)S(1)}, u32[]{:S(2)}, u32[]{:S(2)}) async-start(bf16[8,264,128]{2,1,0:T(8,128)(2,1)} %attend.3), calls=%async_computation.3 | async-start | bytes 1081344 | tf_op jit(solution)/shard_map/all_to_all | solution.py:368
  110.6 0.0 copy-start.4
  110.6 22.3 %attend.2 = bf16[8,264,128]{2,1,0:T(8,128)(2,1)} custom-call(s32[37]{0:T(128)S(1)} %get-tuple-element.7.slots, bf16[8,2,16,1024]{3,2,1,0:T(8,128)(2,1)S(1)} %all-to-all-done.queries, bf16[4096,256]{1,0:T(8,128)(2,1)S(1)} %bitcast.12, bf16[2,128,4096]{2,1,0:T(8,128)(2,1)} %copy-done.5), custom_call_target="tpu_custom_call" | custom-call | flops 10000000000 | bytes 4194304 | tf_op jit(solution)/shard_map/attend/pallas_call | solution.py:344
  132.9 0.0 all-to-all-done.3.returned
  132.9 60.4 %all-to-all-start.1 = ((bf16[8,264,128]{2,1,0:T(8,128)(2,1)}), bf16[8,264,128]{2,1,0:T(8,128)(2,1)S(1)}, u32[]{:S(2)}, u32[]{:S(2)}) async-start(bf16[8,264,128]{2,1,0:T(8,128)(2,1)} %attend.2), calls=%async_computation.1 | async-start | bytes 1081344 | tf_op jit(solution)/shard_map/all_to_all | solution.py:368
  193.3 0.0 copy-done.4
  193.3 1.0 combine.2.rest_0_
  194.3 12.9 %all-to-all-done.1.returned = bf16[8,264,128]{2,1,0:T(8,128)(2,1)S(1)} async-done(((bf16[8,264,128]{2,1,0:T(8,128)(2,1)}), bf16[8,264,128]{2,1,0:T(8,128)(2,1)S(1)}, u32[]{:S(2)}, u32[]{:S(2)}) %all-to-all-start.1) | async-done | bytes 540704 | tf_op jit(solution)/shard_map/all_to_all | solution.py:368
  207.2 1.7 combine.3
Async XLA Ops:
  1.7 21.8 %all-to-all-start.2 = ((bf16[8,2,16,1024]{3,2,1,0:T(8,128)(2,1)}), bf16[8,2,16,1024]{3,2,1,0:T(8,128)(2,1)S(1)}, u32[]{:S(2)}, u32[]{:S(2)}) async-start(bf16[8,2,16,1024]{3,2,1,0:T(8,128)(2,1)} %broadcast_in_dim.24), calls=%async_computation.2 | async-start | bytes 1048576 | tf_op jit(solution)/shard_map/all_to_all | solution.py:338
  10.6 1.6 copy-start
  12.2 0.7 copy-start.2
  12.8 0.7 copy-start.3
  13.5 14.5 %copy-start.1 = (bf16[1,4096,256]{2,1,0:T(8,128)(2,1)S(1)}, bf16[1,4096,256]{2,1,0:T(8,128)(2,1)}, u32[]{:S(2)}) copy-start(bf16[1,4096,256]{2,1,0:T(8,128)(2,1)} %param.7) | copy-start | bytes 6291460
  16.3 1.3 copy-start.5
  24.3 25.9 %all-to-all-start = ((bf16[8,2,16,1024]{3,2,1,0:T(8,128)(2,1)}), bf16[8,2,16,1024]{3,2,1,0:T(8,128)(2,1)S(1)}, u32[]{:S(2)}, u32[]{:S(2)}) async-start(bf16[8,2,16,1024]{3,2,1,0:T(8,128)(2,1)} %broadcast_in_dim.22), calls=%async_computation | async-start | bytes 1048576 | tf_op jit(solution)/shard_map/all_to_all | solution.py:338
  50.3 82.6 %all-to-all-start.3 = ((bf16[8,264,128]{2,1,0:T(8,128)(2,1)}), bf16[8,264,128]{2,1,0:T(8,128)(2,1)S(1)}, u32[]{:S(2)}, u32[]{:S(2)}) async-start(bf16[8,264,128]{2,1,0:T(8,128)(2,1)} %attend.3), calls=%async_computation.3 | async-start | bytes 1081344 | tf_op jit(solution)/shard_map/all_to_all | solution.py:368
  110.6 82.7 %copy-start.4 = (s32[8]{0:T(128)S(1)}, s32[8]{0:T(128)}, u32[]{:S(2)}) copy-start(s32[8]{0:T(128)} %block_place.5) | copy-start | bytes 100
  132.9 74.3 %all-to-all-start.1 = ((bf16[8,264,128]{2,1,0:T(8,128)(2,1)}), bf16[8,264,128]{2,1,0:T(8,128)(2,1)S(1)}, u32[]{:S(2)}, u32[]{:S(2)}) async-start(bf16[8,264,128]{2,1,0:T(8,128)(2,1)} %attend.2), calls=%async_computation.1 | async-start | bytes 1081344 | tf_op jit(solution)/shard_map/all_to_all | solution.py:368

commit v7 on v6

--- a/solution.py
+++ b/solution.py
@@ -157,6 +157,10 @@
         for unit in range(2):
             score_step(unit, first % 2, 0)
 
+        @pl.when(first == 0)
+        def _():
+            copy.wait()
+
         def body(pair, carry):
             place = pair % 2
             limits = limits_of(pair) if masked else None
@@ -236,7 +240,9 @@
         return carry
 
     def every(*accumulators):
-        copy.wait()
+        @pl.when(slots[1] == 0)
+        def _():
+            copy.wait()
 
         @pl.when(slots[0] > 0)
         def _():

time: 210 us -> 209 us (level)
  no operation moved by 1% of the time
where the time goes in v7:
time: 209 us; the launch traced here: 208 us
  starting transfers between devices  132 us (63%)
  Pallas kernels  49.6 us (24%)
  waiting for transfers between devices  18.7 us (9%)
  local copies, waits for them, and re-layouts  8.42 us (4%)
    all_to_all x2, starting transfers between devices, local(): lax.all_to_all(partial, 'seq', split_axis=0, concat_axis=0, tiled=True)  121 us
    pallas_call x2, Pallas kernels, local(): pl.pallas_call(functools.partial(attend, tiles=tiles, head=head), out_sha...  44.1 us
    all_to_all x2, waiting for transfers between devices, local(): lax.all_to_all(partial, 'seq', split_axis=0, concat_axis=0, tiled=True)  12.9 us
    all_to_all x2, starting transfers between devices, local(): lax.all_to_all(outgoing, 'seq', split_axis=0, concat_axis=0, tiled=True)  10.9 us
    all_to_all x2, waiting for transfers between devices, local(): lax.all_to_all(outgoing, 'seq', split_axis=0, concat_axis=0, tiled=True)  5.8 us
    unnamed x13, local copies, waits for them, and re-layouts  5 us
  transfers between devices with their start and end apart: 4, of which 2 were waited for; matrix products, arithmetic and copies ran while one was open for 1% of the time, Pallas kernels for 23%

profile of v7, /device:TPU:0, one launch (start us, length us, event | category | flops | bytes accessed | tf_op | source)
XLA Modules:
  0.0 208.5 jit_solution(12652221910676327123)
XLA Ops:
  0.0 0.8 slice_bitcast_fusion.1
  0.8 0.9 broadcast_in_dim.24
  1.7 7.3 %all-to-all-start.2 = ((bf16[8,2,16,1024]{3,2,1,0:T(8,128)(2,1)}), bf16[8,2,16,1024]{3,2,1,0:T(8,128)(2,1)S(1)}, u32[]{:S(2)}, u32[]{:S(2)}) async-start(bf16[8,2,16,1024]{3,2,1,0:T(8,128)(2,1)} %broadcast_in_dim.24), calls=%async_computation.2 | async-start | bytes 1048576 | tf_op jit(solution)/shard_map/all_to_all | solution.py:344
  9.0 0.8 copy.9.tile_blocks
  9.7 0.8 slice_bitcast_fusion
  10.6 0.0 copy-start
  10.6 1.6 copy-done
  12.2 0.0 copy-start.2
  12.2 0.7 copy-done.2
  12.8 0.0 copy-start.3
  12.8 0.7 copy-done.3
  13.5 0.0 copy-start.1
  13.5 2.8 %prepare.1 = (bf16[2,128,4096]{2,1,0:T(8,128)(2,1)S(1)}, s32[37]{0:T(128)S(1)}) custom-call(s32[1]{0:T(128)} %bitcast.me, s32[16,4]{1,0:T(8,128)S(1)} %copy.9.tile_blocks, s32[8]{0:T(128)S(1)} %copy-done.3, s32[16]{0:T(128)S(1)} %copy-done.2, bf16[4096,256]{1,0:T(8,128)(2,1)S(1)} %bitcast.10), custom_call_target="tpu_custom_call" | custom-call | flops 10000000000 | bytes 4194304 | tf_op jit(solution)/shard_map/prepare/pallas_call | solution.py:326
  16.3 0.0 copy-start.5
  16.3 1.3 copy-done.5
  17.7 5.8 %all-to-all-done.2.queries = bf16[8,2,16,1024]{3,2,1,0:T(8,128)(2,1)S(1)} async-done(((bf16[8,2,16,1024]{3,2,1,0:T(8,128)(2,1)}), bf16[8,2,16,1024]{3,2,1,0:T(8,128)(2,1)S(1)}, u32[]{:S(2)}, u32[]{:S(2)}) %all-to-all-start.2) | async-done | bytes 524320 | tf_op jit(solution)/shard_map/all_to_all | solution.py:344
  23.5 0.9 broadcast_in_dim.22
  24.3 3.6 %all-to-all-start = ((bf16[8,2,16,1024]{3,2,1,0:T(8,128)(2,1)}), bf16[8,2,16,1024]{3,2,1,0:T(8,128)(2,1)S(1)}, u32[]{:S(2)}, u32[]{:S(2)}) async-start(bf16[8,2,16,1024]{3,2,1,0:T(8,128)(2,1)} %broadcast_in_dim.22), calls=%async_computation | async-start | bytes 1048576 | tf_op jit(solution)/shard_map/all_to_all | solution.py:344
  28.0 0.0 copy-done.1
  28.0 22.1 %attend.3 = bf16[8,264,128]{2,1,0:T(8,128)(2,1)} custom-call(s32[37]{0:T(128)S(1)} %get-tuple-element.7.slots, bf16[8,2,16,1024]{3,2,1,0:T(8,128)(2,1)S(1)} %all-to-all-done.2.queries, bf16[4096,256]{1,0:T(8,128)(2,1)S(1)} %bitcast.11, bf16[2,128,4096]{2,1,0:T(8,128)(2,1)} %copy-done.5), custom_call_target="tpu_custom_call" | custom-call | flops 10000000000 | bytes 4194304 | tf_op jit(solution)/shard_map/attend/pallas_call | solution.py:350
  50.1 0.0 all-to-all-done.queries
  50.1 60.3 %all-to-all-start.3 = ((bf16[8,264,128]{2,1,0:T(8,128)(2,1)}), bf16[8,264,128]{2,1,0:T(8,128)(2,1)S(1)}, u32[]{:S(2)}, u32[]{:S(2)}) async-start(bf16[8,264,128]{2,1,0:T(8,128)(2,1)} %attend.3), calls=%async_computation.3 | async-start | bytes 1081344 | tf_op jit(solution)/shard_map/all_to_all | solution.py:374
  110.4 0.0 copy-start.4
  110.4 22.1 %attend.2 = bf16[8,264,128]{2,1,0:T(8,128)(2,1)} custom-call(s32[37]{0:T(128)S(1)} %get-tuple-element.7.slots, bf16[8,2,16,1024]{3,2,1,0:T(8,128)(2,1)S(1)} %all-to-all-done.queries, bf16[4096,256]{1,0:T(8,128)(2,1)S(1)} %bitcast.12, bf16[2,128,4096]{2,1,0:T(8,128)(2,1)} %copy-done.5), custom_call_target="tpu_custom_call" | custom-call | flops 10000000000 | bytes 4194304 | tf_op jit(solution)/shard_map/attend/pallas_call | solution.py:350
  132.5 0.0 all-to-all-done.3.returned
  132.5 60.5 %all-to-all-start.1 = ((bf16[8,264,128]{2,1,0:T(8,128)(2,1)}), bf16[8,264,128]{2,1,0:T(8,128)(2,1)S(1)}, u32[]{:S(2)}, u32[]{:S(2)}) async-start(bf16[8,264,128]{2,1,0:T(8,128)(2,1)} %attend.2), calls=%async_computation.1 | async-start | bytes 1081344 | tf_op jit(solution)/shard_map/all_to_all | solution.py:374
  192.9 0.0 copy-done.4
  192.9 1.0 combine.2.rest_0_
  193.9 12.9 %all-to-all-done.1.returned = bf16[8,264,128]{2,1,0:T(8,128)(2,1)S(1)} async-done(((bf16[8,264,128]{2,1,0:T(8,128)(2,1)}), bf16[8,264,128]{2,1,0:T(8,128)(2,1)S(1)}, u32[]{:S(2)}, u32[]{:S(2)}) %all-to-all-start.1) | async-done | bytes 540704 | tf_op jit(solution)/shard_map/all_to_all | solution.py:374
  206.8 1.7 combine.3
Async XLA Ops:
  1.7 21.8 %all-to-all-start.2 = ((bf16[8,2,16,1024]{3,2,1,0:T(8,128)(2,1)}), bf16[8,2,16,1024]{3,2,1,0:T(8,128)(2,1)S(1)}, u32[]{:S(2)}, u32[]{:S(2)}) async-start(bf16[8,2,16,1024]{3,2,1,0:T(8,128)(2,1)} %broadcast_in_dim.24), calls=%async_computation.2 | async-start | bytes 1048576 | tf_op jit(solution)/shard_map/all_to_all | solution.py:344
  10.6 1.6 copy-start
  12.2 0.7 copy-start.2
  12.8 0.7 copy-start.3
  13.5 14.5 %copy-start.1 = (bf16[1,4096,256]{2,1,0:T(8,128)(2,1)S(1)}, bf16[1,4096,256]{2,1,0:T(8,128)(2,1)}, u32[]{:S(2)}) copy-start(bf16[1,4096,256]{2,1,0:T(8,128)(2,1)} %param.7) | copy-start | bytes 6291460
  16.3 1.3 copy-start.5
  24.3 25.7 %all-to-all-start = ((bf16[8,2,16,1024]{3,2,1,0:T(8,128)(2,1)}), bf16[8,2,16,1024]{3,2,1,0:T(8,128)(2,1)S(1)}, u32[]{:S(2)}, u32[]{:S(2)}) async-start(bf16[8,2,16,1024]{3,2,1,0:T(8,128)(2,1)} %broadcast_in_dim.22), calls=%async_computation | async-start | bytes 1048576 | tf_op jit(solution)/shard_map/all_to_all | solution.py:344
  50.1 82.4 %all-to-all-start.3 = ((bf16[8,264,128]{2,1,0:T(8,128)(2,1)}), bf16[8,264,128]{2,1,0:T(8,128)(2,1)S(1)}, u32[]{:S(2)}, u32[]{:S(2)}) async-start(bf16[8,264,128]{2,1,0:T(8,128)(2,1)} %attend.3), calls=%async_computation.3 | async-start | bytes 1081344 | tf_op jit(solution)/shard_map/all_to_all | solution.py:374
  110.4 82.5 %copy-start.4 = (s32[8]{0:T(128)S(1)}, s32[8]{0:T(128)}, u32[]{:S(2)}) copy-start(s32[8]{0:T(128)} %block_place.5) | copy-start | bytes 100
  132.5 74.3 %all-to-all-start.1 = ((bf16[8,264,128]{2,1,0:T(8,128)(2,1)}), bf16[8,264,128]{2,1,0:T(8,128)(2,1)S(1)}, u32[]{:S(2)}, u32[]{:S(2)}) async-start(bf16[8,264,128]{2,1,0:T(8,128)(2,1)} %attend.2), calls=%async_computation.1 | async-start | bytes 1081344 | tf_op jit(solution)/shard_map/all_to_all | solution.py:374
